TPU v7x, 32 devices: a whole 2x2x4 slice. The times are simulated.
32 devices in a mesh: dp: 2 (over x), tp: 4 (over z), cp: 4 (over y, core).
Axes of the slice: x: 2, y: 2, z: 4, core: 2. Of those that a mesh axis runs over, the one named last changes fastest.
Arguments:
- hidden: bfloat16 [8192, 4096], P(('dp', 'cp')), parts along dimension 0
- tok_pos: int32 [8192], P(('dp', 'cp')), parts along dimension 0
- norm_gain: float32 [4096], replicated
- w_query: bfloat16 [4096, 4096], P(None, 'tp')
- w_key: bfloat16 [4096, 1024], P(None, 'tp')
- w_value: bfloat16 [4096, 1024], P(None, 'tp')
- w_out: bfloat16 [4096, 4096], P('tp')
Outputs:
- output 1: bfloat16 [8192, 4096], P(('dp', 'cp')), parts along dimension 0
- output 2: bfloat16 [8192, 8, 128], P(('dp', 'cp'), 'tp'), parts along dimension 0
- output 3: bfloat16 [8192, 8, 128], P(('dp', 'cp'), 'tp'), parts along dimension 0
There are 2 independent parts. A program takes and returns all parts, laid end to end along the dimension named above; an argument that names none is the same for every part.
All inputs are finite; a program needn't handle non-finite values.
Results may differ from a plain program's by a relative error of at most 0.00439956.
Values are sent between devices in bfloat16 or wider.
A program may use at most 1 GiB of HBM per device.

v0:
```python
import functools
import math

import jax
import jax.numpy as jnp
from jax import lax
from jax.experimental import pallas as pl
from jax.experimental.pallas import tpu as pltpu
from jax.sharding import PartitionSpec as P

HEAD = 128
THETA = 1000000
EPS = 1e-5
NEG_BIG = -1e30
KB = 128
GROUP = 4
QB = 128


def rope_tables(tok_pos):
    inv_freq = 1.0 / (THETA ** (jnp.arange(0, HEAD, 2, dtype=jnp.float32) / HEAD))
    inv_freq = jnp.concatenate([inv_freq, inv_freq])
    sign = jnp.where(jnp.arange(HEAD) < HEAD // 2, -1.0, 1.0).astype(jnp.float32)
    angles = tok_pos.astype(jnp.float32)[:, None] * inv_freq[None, :]
    return jnp.cos(angles), jnp.sin(angles) * sign[None, :]


def rotate(x_f32, cos_tab, sin_tab):
    x = x_f32.astype(jnp.bfloat16).astype(jnp.float32)
    return (x * cos_tab + pltpu.roll(x, HEAD // 2, 1) * sin_tab).astype(jnp.bfloat16)


def kv_kernel(x_ref, gain_ref, wk_ref, wv_ref, cos_ref, sin_ref, normed_ref, kv_ref):
    x = x_ref[...].astype(jnp.float32)
    var = jnp.mean(x * x, axis=-1, keepdims=True)
    normed = (x * lax.rsqrt(var + EPS) * gain_ref[...]).astype(jnp.bfloat16)
    normed_ref[...] = normed
    n_k = wk_ref.shape[1]
    k = jnp.dot(normed, wk_ref[...], preferred_element_type=jnp.float32)
    v = jnp.dot(normed, wv_ref[...], preferred_element_type=jnp.float32)
    for h in range(n_k // HEAD):
        cols = slice(h * HEAD, (h + 1) * HEAD)
        kv_ref[:, cols] = rotate(k[:, cols], cos_ref[...], sin_ref[...])
    kv_ref[:, n_k:] = v.astype(jnp.bfloat16)


def q_kernel(normed_ref, wq_ref, cos_ref, sin_ref, q_ref):
    for c in range(0, wq_ref.shape[1], 2 * HEAD):
        q = jnp.dot(normed_ref[...], wq_ref[:, c:c + 2 * HEAD], preferred_element_type=jnp.float32)
        for h in range(2):
            q_ref[:, c + h * HEAD:c + (h + 1) * HEAD] = rotate(q[:, h * HEAD:(h + 1) * HEAD], cos_ref[...], sin_ref[...])


def attn_kernel(head, n_kv, kmin_ref, kmax_ref, qmin_ref, qmax_ref, q_ref, posq_ref, posk_ref, kv0, kv1, kv2, kv3, o_ref,
                k_s, v_s, q_s, pq_s, m_s, l_s, acc_s, full_l, part_l, sems):
    step = pl.program_id(0)
    rows = kv0.shape[0]
    n_blocks = kmin_ref.shape[0]
    n_heads = q_ref.shape[1] // HEAD

    @pl.when(step == 0)
    def _():
        copies = []
        for i, src in enumerate((kv0, kv1, kv2, kv3)):
            copies.append(pltpu.make_async_copy(src.at[:, pl.ds(head * HEAD, HEAD)], k_s.at[pl.ds(i * rows, rows), :], sems.at[2 * i]))
            copies.append(pltpu.make_async_copy(src.at[:, pl.ds((n_kv + head) * HEAD, HEAD)], v_s.at[pl.ds(i * rows, rows), :], sems.at[2 * i + 1]))
        for c in copies:
            c.start()
        for c in copies:
            c.wait()

    q_lo = qmin_ref[step]
    q_hi = qmax_ref[step]

    def classify(j, counts):
        n_full, n_part = counts
        lo, hi = kmin_ref[j], kmax_ref[j]
        is_full = hi <= q_lo
        is_part = jnp.logical_and(lo <= q_hi, jnp.logical_not(is_full))

        @pl.when(is_full)
        def _():
            full_l[n_full] = j

        @pl.when(is_part)
        def _():
            part_l[n_part] = j

        return n_full + is_full.astype(jnp.int32), n_part + is_part.astype(jnp.int32)

    n_full, n_part = lax.fori_loop(0, n_blocks, classify, (0, 0))
    n_groups = n_full // GROUP

    def move(i, n_part):
        part_l[n_part] = full_l[n_groups * GROUP + i]
        return n_part + 1

    n_part = lax.fori_loop(0, n_full - n_groups * GROUP, move, n_part)
    n_mgroups = (n_part + GROUP - 1) // GROUP

    def pad(i, _):
        part_l[n_part + i] = 0
        return 0

    lax.fori_loop(0, n_mgroups * GROUP - n_part, pad, 0)

    for h in range(n_heads):
        q_s[h * QB:(h + 1) * QB, :] = q_ref[:, h * HEAD:(h + 1) * HEAD]
        pq_s[h * QB:(h + 1) * QB, :] = posq_ref[...]
    m_s[...] = jnp.full_like(m_s, NEG_BIG)
    l_s[...] = jnp.zeros_like(l_s)
    acc_s[...] = jnp.zeros_like(acc_s)

    scale = HEAD ** -0.5 * math.log2(math.e)
    half = n_heads * QB // 2

    def absorb(blocks, pos_row):
        k = jnp.concatenate([k_s[pl.ds(pl.multiple_of(b * KB, KB), KB), :] for b in blocks], axis=0)
        v = jnp.concatenate([v_s[pl.ds(pl.multiple_of(b * KB, KB), KB), :] for b in blocks], axis=0)
        for part in range(2):
            sl = slice(part * half, (part + 1) * half)
            s = lax.dot_general(q_s[sl, :], k, (((1,), (1,)), ((), ())), preferred_element_type=jnp.float32) * scale
            if pos_row is not None:
                s = jnp.where(pos_row <= pq_s[sl, :], s, NEG_BIG)
            m_old = m_s[sl, :]
            m_new = jnp.maximum(m_old, jnp.max(s, axis=-1, keepdims=True))
            alpha = jnp.exp2(m_old - m_new)
            p = jnp.exp2(s - m_new)
            l_new = p[:, :HEAD]
            for c in range(1, GROUP):
                l_new = l_new + p[:, c * HEAD:(c + 1) * HEAD]
            l_s[sl, :] = l_s[sl, :] * alpha + l_new
            acc_s[sl, :] = acc_s[sl, :] * alpha + jnp.dot(p.astype(jnp.bfloat16), v, preferred_element_type=jnp.float32)
            m_s[sl, :] = m_new

    def full_step(i, _):
        absorb([full_l[i * GROUP + c] for c in range(GROUP)], None)
        return 0

    lax.fori_loop(0, n_groups, full_step, 0)

    def part_step(i, _):
        blocks = [part_l[i * GROUP + c] for c in range(GROUP)]
        rows_pos = [posk_ref[b] + jnp.where(i * GROUP + c < n_part, 0, 1 << 30) for c, b in enumerate(blocks)]
        absorb(blocks, jnp.concatenate(rows_pos, axis=1))
        return 0

    lax.fori_loop(0, n_mgroups, part_step, 0)

    out = (acc_s[...] / jnp.sum(l_s[...], axis=-1, keepdims=True)).astype(jnp.bfloat16)
    for h in range(n_heads):
        o_ref[:, h * HEAD:(h + 1) * HEAD] = out[h * QB:(h + 1) * QB, :]

TILE = 512
CHUNK = 256


def out_kernel(n_tp, n_cp, o_hbm, w_hbm, z_hbm, x_hbm, out_hbm, o_buf, w_buf, acc, w_t, x_t, y_t,
               o_send, o_recv, w_send, w_recv, w_local, ld_sem, st_sem, own_sem):
    mesh_id = pl.DeviceIdType.MESH
    tp, dp, cp = lax.axis_index("tp"), lax.axis_index("dp"), lax.axis_index("cp")
    core, chip = cp % 2, cp // 2
    cp_y = cp + 2 - 4 * chip
    to_right, to_left = {"tp": (tp + 1) % n_tp}, {"tp": (tp + n_tp - 1) % n_tp}
    to_x, to_y, to_p = {"dp": 1 - dp}, {"cp": cp_y}, {"cp": cp + 1 - 2 * core}
    p_me, p_x, p_y, p_d = dp * n_cp + cp, (1 - dp) * n_cp + cp, dp * n_cp + cp_y, (1 - dp) * n_cp + cp_y
    sl = z_hbm.shape[1]
    width = acc.shape[1]
    n_chunk = o_buf.shape[2] // CHUNK
    n_tile = width // TILE

    barrier = pltpu.get_barrier_semaphore()
    for peer in (to_right, to_left, to_x, to_y, to_p):
        pl.semaphore_signal(barrier, inc=1, device_id=peer, device_id_type=mesh_id)
    pl.semaphore_wait(barrier, 5)

    def o_copy(s, c):
        cols = pl.ds(c * CHUNK, CHUNK)
        src = o_hbm.at[:, cols] if s == 0 else o_buf.at[s, :, cols]
        return pltpu.make_async_remote_copy(src_ref=src, dst_ref=o_buf.at[s + 1, :, cols], send_sem=o_send.at[s, c],
                                            recv_sem=o_recv.at[s, c], device_id=to_right, device_id_type=mesh_id)

    def rows(p, first=0, n=None):
        return pl.ds(pl.multiple_of(p * sl + first, sl // 2), sl if n is None else n)

    def w_copy(k, kind):
        half = sl // 2
        own = z_hbm.at[(tp + n_tp - k - 1) % n_tp]
        idx, peer, where = {
            "own_x": (0, to_x, rows(p_me)), "own_y": (1, to_y, rows(p_me)), "own_p": (2, to_p, rows(p_me)),
            "dx": (3, to_x, rows(p_y, half, half)), "dy": (4, to_y, rows(p_x, 0, half)),
            "px": (5, to_p, rows(p_x)), "py": (6, to_p, rows(p_y)),
            "pd0": (7, to_p, rows(p_d, 0, half)), "pd1": (8, to_p, rows(p_d, half, half)),
        }[kind]
        src = own if idx < 3 else w_buf.at[k, where, :]
        return pltpu.make_async_remote_copy(src_ref=src, dst_ref=w_buf.at[k, where, :], send_sem=w_send.at[k, idx],
                                            recv_sem=w_recv.at[k, idx], device_id=peer, device_id_type=mesh_id)

    def w_own_local(k):
        return pltpu.make_async_copy(z_hbm.at[(tp + n_tp - k - 1) % n_tp], w_buf.at[k, rows(p_me), :], w_local.at[k])

    def start_own(k):
        for kind in ("own_x", "own_y", "own_p"):
            w_copy(k, kind).start()
        w_own_local(k).start()

    def pass_on(k):
        w_copy(k, "own_x").wait_recv()
        w_copy(k, "own_y").wait_recv()
        for kind in ("dx", "dy", "px", "py"):
            w_copy(k, kind).start()

    def pass_diag(k):
        w_copy(k, "dy").wait_recv()
        w_copy(k, "pd0").start()
        w_copy(k, "dx").wait_recv()
        w_copy(k, "pd1").start()

    def complete(k):
        w_own_local(k).wait()
        for kind in ("own_p", "px", "py", "pd0", "pd1"):
            w_copy(k, kind).wait_recv()

    def arrive(s, c):
        o_copy(s, c).wait_recv()
        if s + 1 < n_tp - 1:
            o_copy(s + 1, c).start()

    def tile_cols(t):
        return pl.ds(pl.multiple_of(t * TILE, TILE), TILE)

    def accum(s, k0, k1):
        def body(t, _):
            cols = tile_cols(t)
            acc[:, cols] += jnp.dot(o_buf[s, :, k0:k1], w_buf[s - 1, k0:k1, cols], preferred_element_type=jnp.float32)
            return 0

        lax.fori_loop(0, n_tile, body, 0)

    for c in range(n_chunk):
        o_copy(0, c).start()
    start_own(0)
    own = pltpu.make_async_copy(o_hbm, o_buf.at[0], own_sem)
    own.start()

    def loads(t, slot):
        cols = tile_cols(t)
        return (pltpu.make_async_copy(w_hbm.at[:, cols], w_t.at[slot], ld_sem.at[slot, 0]),
                pltpu.make_async_copy(x_hbm.at[:, cols], x_t.at[slot], ld_sem.at[slot, 1]))

    for d in loads(0, 0):
        d.start()
    own.wait()

    def first(t, _):
        slot = t % 2

        @pl.when(t + 1 < n_tile)
        def _():
            for d in loads(t + 1, (t + 1) % 2):
                d.start()

        for d in loads(t, slot):
            d.wait()
        acc[:, tile_cols(t)] = x_t[slot].astype(jnp.float32) + jnp.dot(o_buf[0], w_t[slot], preferred_element_type=jnp.float32)
        return 0

    lax.fori_loop(0, n_tile, first, 0)

    half_k = n_chunk * CHUNK // 2
    for s in range(1, n_tp):
        last = s == n_tp - 1
        pass_on(s - 1)
        if not last:
            start_own(s)
        arrive(s - 1, 0)
        arrive(s - 1, 1)
        pass_diag(s - 1)
        if not last:
            arrive(s - 1, 2)
        complete(s - 1)
        accum(s, 0, half_k)
        if last:
            arrive(s - 1, 2)
            accum(s, half_k, half_k + CHUNK)
        arrive(s - 1, 3)
        if not last:
            accum(s, half_k, 2 * half_k)

    def store(t, slot):
        return pltpu.make_async_copy(y_t.at[slot], out_hbm.at[:, tile_cols(t)], st_sem.at[slot])

    k0 = half_k + CHUNK

    def final(t, _):
        slot = t % 2

        @pl.when(t >= 2)
        def _():
            store(t - 2, slot).wait()

        cols = tile_cols(t)
        y = acc[:, cols] + jnp.dot(o_buf[n_tp - 1, :, k0:], w_buf[n_tp - 2, k0:, cols], preferred_element_type=jnp.float32)
        y_t[slot] = y.astype(jnp.bfloat16)
        store(t, slot).start()
        return 0

    lax.fori_loop(0, n_tile, final, 0)
    store(n_tile - 2, n_tile % 2).wait()
    store(n_tile - 1, (n_tile - 1) % 2).wait()
    for s in range(n_tp - 1):
        for c in range(n_chunk):
            o_copy(s, c).wait_send()
        for kind in ("own_x", "own_y", "own_p", "dx", "dy", "px", "py", "pd0", "pd1"):
            w_copy(s, kind).wait_send()


def solution(mesh):
    n_tp, n_cp, n_dp = mesh.shape["tp"], mesh.shape["cp"], mesh.shape["dp"]
    plane = n_dp * n_cp
    swap_core = [(i, i ^ 1) for i in range(n_cp)]
    swap_chip = [(i, i ^ 2) for i in range(n_cp)]

    def local_block(hidden, tok_pos, norm_gain, w_query, w_key, w_value, w_out):
        rows, width = hidden.shape
        q_cols, k_cols = w_query.shape[1], w_key.shape[1]
        n_kv = k_cols // HEAD
        g_cols = q_cols // n_kv
        plane_idx = lax.axis_index("dp") * n_cp + lax.axis_index("cp")

        slice_rows = w_out.shape[0] // plane
        own_slice = lax.dynamic_slice_in_dim(w_out, plane_idx * slice_rows, slice_rows, axis=0)
        z_slices = lax.all_gather(own_slice, "tp", axis=0, tiled=False)

        cos_tab, sin_tab = rope_tables(tok_pos)
        rb = 256
        row_blk = lambda cols: pl.BlockSpec((rb, cols), lambda i: (i, 0))
        whole = lambda r, c: pl.BlockSpec((r, c), lambda i: (0, 0))
        normed, kv = pl.pallas_call(
            kv_kernel,
            grid=(rows // rb,),
            out_shape=(jax.ShapeDtypeStruct((rows, width), jnp.bfloat16), jax.ShapeDtypeStruct((rows, 2 * k_cols), jnp.bfloat16)),
            in_specs=[row_blk(width), whole(1, width), whole(width, k_cols), whole(width, k_cols), row_blk(HEAD), row_blk(HEAD)],
            out_specs=(row_blk(width), row_blk(2 * k_cols)),
            cost_estimate=pl.CostEstimate(flops=4 * rows * width * k_cols, bytes_accessed=24 << 20, transcendentals=0),
            name="norm_kv",
        )(hidden, norm_gain.reshape(1, width), w_key, w_value, cos_tab, sin_tab)

        pos_row = tok_pos.reshape(rows // KB, 1, KB)
        kv_core = lax.ppermute(kv, "cp", swap_core)
        kv_chip = lax.ppermute(kv, "cp", swap_chip)
        swap_diag = [(i, i ^ 3) for i in range(n_cp)]
        pos_rel = jnp.concatenate([pos_row] + [lax.ppermute(pos_row, "cp", pairs) for pairs in (swap_core, swap_chip, swap_diag)], axis=0)

        q_rot = pl.pallas_call(
            q_kernel,
            grid=(rows // rb,),
            out_shape=jax.ShapeDtypeStruct((rows, q_cols), jnp.bfloat16),
            in_specs=[row_blk(width), whole(width, q_cols), row_blk(HEAD), row_blk(HEAD)],
            out_specs=row_blk(q_cols),
            cost_estimate=pl.CostEstimate(flops=2 * rows * width * q_cols, bytes_accessed=20 << 20, transcendentals=0),
            name="q_rope",
        )(normed, w_query, cos_tab, sin_tab)

        kv_chip, q_rot = lax.optimization_barrier((kv_chip, q_rot))
        kv_diag = lax.ppermute(kv_chip, "cp", swap_core)

        kmin, kmax = jnp.min(pos_rel, axis=(1, 2)), jnp.max(pos_rel, axis=(1, 2))
        n_q = rows // QB
        qpos = tok_pos.reshape(n_q, QB)
        qmin, qmax = jnp.min(qpos, axis=1), jnp.max(qpos, axis=1)
        pos_col = tok_pos.reshape(rows, 1)
        hq = g_cols // HEAD
        smem = pl.BlockSpec(memory_space=pltpu.SMEM)
        anym = pl.BlockSpec(memory_space=pl.ANY)

        def attend(head):
            return pl.pallas_call(
                functools.partial(attn_kernel, head, n_kv),
                grid=(n_q,),
                out_shape=jax.ShapeDtypeStruct((rows, g_cols), jnp.bfloat16),
                in_specs=[smem] * 4 + [pl.BlockSpec((QB, g_cols), lambda i: (i, head)), pl.BlockSpec((QB, 1), lambda i: (i, 0)),
                                       pl.BlockSpec(pos_rel.shape, lambda i: (0, 0, 0))] + [anym] * 4,
                out_specs=pl.BlockSpec((QB, g_cols), lambda i: (i, 0)),
                scratch_shapes=[
                    pltpu.VMEM((n_cp * rows, HEAD), jnp.bfloat16),
                    pltpu.VMEM((n_cp * rows, HEAD), jnp.bfloat16),
                    pltpu.VMEM((hq * QB, HEAD), jnp.bfloat16),
                    pltpu.VMEM((hq * QB, 1), jnp.int32),
                    pltpu.VMEM((hq * QB, 1), jnp.float32),
                    pltpu.VMEM((hq * QB, HEAD), jnp.float32),
                    pltpu.VMEM((hq * QB, HEAD), jnp.float32),
                    pltpu.SMEM((n_cp * rows // KB + GROUP,), jnp.int32),
                    pltpu.SMEM((n_cp * rows // KB + 2 * GROUP,), jnp.int32),
                    pltpu.SemaphoreType.DMA((8,)),
                ],
                cost_estimate=pl.CostEstimate(flops=4 * rows * n_cp * rows * g_cols, bytes_accessed=8 << 20, transcendentals=0),
                name="attend",
            )(kmin, kmax, qmin, qmax, q_rot, pos_col, pos_rel, kv, kv_core, kv_chip, kv_diag)

        o = jnp.concatenate([attend(g) for g in range(n_kv)], axis=1)
        n_chunk = q_cols // CHUNK
        sl = w_out.shape[0] // plane
        hidden_out = pl.pallas_call(
            functools.partial(out_kernel, n_tp, n_cp),
            out_shape=jax.ShapeDtypeStruct((rows, width), jnp.bfloat16),
            in_specs=[anym] * 4,
            out_specs=anym,
            scratch_shapes=[
                pltpu.VMEM((n_tp, rows, q_cols), jnp.bfloat16),
                pltpu.VMEM((n_tp - 1, q_cols, width), jnp.bfloat16),
                pltpu.VMEM((rows, width), jnp.float32),
                pltpu.VMEM((2, q_cols, TILE), jnp.bfloat16),
                pltpu.VMEM((2, rows, TILE), jnp.bfloat16),
                pltpu.VMEM((2, rows, TILE), jnp.bfloat16),
                pltpu.SemaphoreType.DMA((n_tp - 1, n_chunk)),
                pltpu.SemaphoreType.DMA((n_tp - 1, n_chunk)),
                pltpu.SemaphoreType.DMA((n_tp - 1, 9)),
                pltpu.SemaphoreType.DMA((n_tp - 1, 9)),
                pltpu.SemaphoreType.DMA((n_tp - 1,)),
                pltpu.SemaphoreType.DMA((2, 2)),
                pltpu.SemaphoreType.DMA((2,)),
                pltpu.SemaphoreType.DMA,
            ],
            compiler_params=pltpu.CompilerParams(collective_id=0, has_side_effects=True, vmem_limit_bytes=63 << 20),
            cost_estimate=pl.CostEstimate(flops=2 * n_tp * rows * q_cols * width, bytes_accessed=48 << 20, transcendentals=0),
            name="out_gather",
        )(o, w_out, z_slices, hidden)
        k_cache = kv[:, :k_cols].reshape(rows, n_kv, HEAD)
        v_cache = kv[:, k_cols:].reshape(rows, n_kv, HEAD)
        return hidden_out, k_cache, v_cache

    row_spec = P(("dp", "cp"), None)
    cache_spec = P(("dp", "cp"), "tp", None)
    return jax.shard_map(local_block, mesh=mesh, in_specs=(row_spec, P(("dp", "cp")), P(None), P(None, "tp"), P(None, "tp"), P(None, "tp"), P("tp", None)), out_specs=(row_spec, cache_spec, cache_spec), check_vma=False)
```

profile of v0, /device:TPU:5, one launch (start us, length us, event | category | flops | bytes accessed | tf_op | source)
XLA Modules:
  0.0 330.0 jit_solution(13505568780319978621)
XLA Ops:
  7.2 0.0 all-gather.3.cloned.1.call-start
  7.2 2.3 constant_dynamic-slice_fusion
  9.5 0.0 all-gather.3.cloned.1.call-update
  9.5 0.7 convert_element_type.3
  10.3 0.1 compare_select_fusion
  10.3 3.0 fusion
  13.4 11.2 %norm_kv.1 = (bf16[1024,4096]{1,0:T(8,128)(2,1)}, bf16[1024,512]{1,0:T(8,128)(2,1)}) custom-call(bf16[1024,4096]{1,0:T(8,128)(2,1)} %x_hbm.1, f32[1,4096]{1,0:T(1,128)} %bitcast.13, bf16[4096,256]{1,0:T(8,128)(2,1)} %wk_ref.1, bf16[4096,256]{1,0:T(8,128)(2,1)} %wv_ref.1, f32[1024,128]{1,0:T(8,128)} %get-tuple-element.19.cos_ref, ...), custom_call_target="tpu_custom_call" | custom-call | flops 4294967296 | bytes 25165824 | tf_op jit(solution)/shard_map/norm_kv/pallas_call | solution.py:339
  24.6 0.7 collective-permute-start.4
  25.3 14.9 %q_rope.1.q_ref = bf16[1024,1024]{1,0:T(8,128)(2,1)} custom-call(bf16[1024,4096]{1,0:T(8,128)(2,1)} %get-tuple-element.8.normed_ref, bf16[4096,1024]{1,0:T(8,128)(2,1)} %wq_ref.1, f32[1024,128]{1,0:T(8,128)} %get-tuple-element.19.cos_ref, f32[1024,128]{1,0:T(8,128)} %get-tuple-element.18.sin_ref), custom_call_target="tpu_custom_call" | custom-call | flops 8589934592 | bytes 20971520 | tf_op jit(solution)/shard_map/q_rope/pallas_call | solution.py:355
  40.3 8.5 %collective-permute-done.3.kv2 = bf16[1024,512]{1,0:T(8,128)(2,1)S(1)} collective-permute-done((bf16[1024,512]{1,0:T(8,128)(2,1)}, bf16[1024,512]{1,0:T(8,128)(2,1)S(1)}, u32[]{:S(2)}, u32[]{:S(2)}) %collective-permute-start.3) | collective-permute-done | bytes 1048608 | tf_op jit(solution)/shard_map/ppermute | solution.py:351
  48.7 1.4 collective-permute-start.5
  50.2 1.4 collective-permute-start.1
  51.6 0.7 collective-permute-start
  52.3 0.1 fusion.2
  52.4 0.7 bitcast_reduce_fusion
  53.1 1.1 copy.12.posq_ref
  54.1 0.9 reshape.36
  55.0 0.9 reshape.35
  56.0 1.8 fusion.1
  57.8 39.8 %attend.3 = bf16[1024,512]{1,0:T(8,128)(2,1)} custom-call(s32[32]{0:T(128)} %get-tuple-element.12.kmin_ref, s32[32]{0:T(128)} %get-tuple-element.11.kmax_ref, s32[8]{0:T(128)} %get-tuple-element.14.qmin_ref, s32[8]{0:T(128)} %get-tuple-element.13.qmax_ref, bf16[1024,1024]{1,0:T(8,128)(2,1)} %q_rope.1.q_ref, s32[1024,1]{1,0:T(8,128)} %copy.12.posq_ref, ...), custom_call_target="tpu_custom_call" | custom-call | flops 8589934592 | bytes 8388608 | tf_op jit(solution)/shard_map/attend/pallas_call | solution.py:378
  97.6 39.9 %attend.2 = bf16[1024,512]{1,0:T(8,128)(2,1)} custom-call(s32[32]{0:T(128)} %get-tuple-element.12.kmin_ref, s32[32]{0:T(128)} %get-tuple-element.11.kmax_ref, s32[8]{0:T(128)} %get-tuple-element.14.qmin_ref, s32[8]{0:T(128)} %get-tuple-element.13.qmax_ref, bf16[1024,1024]{1,0:T(8,128)(2,1)} %q_rope.1.q_ref, s32[1024,1]{1,0:T(8,128)} %copy.12.posq_ref, ...), custom_call_target="tpu_custom_call" | custom-call | flops 8589934592 | bytes 8388608 | tf_op jit(solution)/shard_map/attend/pallas_call | solution.py:378
  137.5 2.9 pad_maximum_fusion.o_hbm
  140.4 174.9 %out_gather.1 = bf16[1024,4096]{1,0:T(8,128)(2,1)} custom-call(bf16[1024,1024]{1,0:T(8,128)(2,1)} %pad_maximum_fusion.o_hbm, bf16[1024,4096]{1,0:T(8,128)(2,1)} %w_hbm.1, bf16[4,128,4096]{2,1,0:T(8,128)(2,1)} %bitcast.12, bf16[1024,4096]{1,0:T(8,128)(2,1)} %x_hbm.1), custom_call_target="tpu_custom_call" | custom-call | flops 34359738368 | bytes 50331648 | tf_op jit(solution)/shard_map/out_gather/pallas_call | solution.py:404
  315.3 7.9 %copy.15 = bf16[1024,4096]{1,0:T(8,128)(2,1)} copy(bf16[1024,4096]{1,0:T(8,128)(2,1)} %out_gather.1) | data formatting | bytes 16777216
  (17 shorter events, 0.0 us)
Async XLA Ops:
  7.2 133.2 %all-gather.3.cloned.1.call-start = ((), (), s32[]{:S(2)}) async-start(), calls=%async_computation | async-start | bytes 5242880 | tf_op jit(solution)/shard_map/all_gather | solution.py:333
  24.6 24.1 %collective-permute-start.3 = (bf16[1024,512]{1,0:T(8,128)(2,1)}, bf16[1024,512]{1,0:T(8,128)(2,1)S(1)}, u32[]{:S(2)}, u32[]{:S(2)}) collective-permute-start(bf16[1024,512]{1,0:T(8,128)(2,1)} %get-tuple-element.7.kv0), channel_id=1, source_target_pairs={{0,2},{1,3},{2,0},{3,1},{4,6},{5,7},{6,4},{7,5},{8,10},{9,11},{10,... | collective-permute-start | bytes 3145736 | tf_op jit(solution)/shard_map/ppermute | solution.py:351
  24.6 33.2 %collective-permute-start.4 = (bf16[1024,512]{1,0:T(8,128)(2,1)}, bf16[1024,512]{1,0:T(8,128)(2,1)}, u32[]{:S(2)}, u32[]{:S(2)}) collective-permute-start(bf16[1024,512]{1,0:T(8,128)(2,1)} %get-tuple-element.7.kv0), channel_id=1, source_target_pairs={{0,1},{1,0},{2,3},{3,2},{4,5},{5,4},{6,7},{7,6},{8,9},{9,8},{10,11... | collective-permute-start | bytes 3145736 | tf_op jit(solution)/shard_map/ppermute | solution.py:350
  25.3 24.8 %copy-start.2 = (s32[1024]{0:T(1024)S(1)}, s32[1024]{0:T(1024)}, u32[]{:S(2)}) copy-start(s32[1024]{0:T(1024)} %param.8) | copy-start | bytes 12292
  25.3 27.0 %copy-start = (bf16[1024,512]{1,0:T(8,128)(2,1)S(1)}, bf16[1024,512]{1,0:T(8,128)(2,1)}, u32[]{:S(2)}) copy-start(bf16[1024,512]{1,0:T(8,128)(2,1)} %get-tuple-element.7.kv0) | copy-start | bytes 3145732
  48.7 9.0 %copy-start.3 = (bf16[1024,512]{1,0:T(8,128)(2,1)}, bf16[1024,512]{1,0:T(8,128)(2,1)S(1)}, u32[]{:S(2)}) copy-start(bf16[1024,512]{1,0:T(8,128)(2,1)S(1)} %collective-permute-done.3.kv2) | copy-start | bytes 3145732
  48.7 9.0 %collective-permute-start.5 = (bf16[1024,512]{1,0:T(8,128)(2,1)S(1)}, bf16[1024,512]{1,0:T(8,128)(2,1)}, u32[]{:S(2)}, u32[]{:S(2)}) collective-permute-start(bf16[1024,512]{1,0:T(8,128)(2,1)S(1)} %collective-permute-done.3.kv2), channel_id=1, source_target_pairs={{0,1},{1,0},{2,3},{3,2},{4,5},{5,4},{6,7},{7,6},{8,9},{9,8},{10,11... | collective-permute-start | bytes 3145736 | tf_op jit(solution)/shard_map/ppermute | solution.py:366
  50.2 5.8 %collective-permute-start.2 = (s32[8,1,128]{2,1,0:T(1,128)S(1)}, s32[8,1,128]{2,1,0:T(1,128)S(1)}, u32[]{:S(2)}, u32[]{:S(2)}) collective-permute-start(s32[8,1,128]{2,1,0:T(1,128)S(1)} %bitcast.7), channel_id=1, source_target_pairs={{0,3},{1,2},{2,1},{3,0},{4,7},{5,6},{6,5},{7,4},{8,11},{9,10},{10,... | collective-permute-start | bytes 12296 | tf_op jit(solution)/shard_map/ppermute | solution.py:353
  50.2 5.8 %collective-permute-start.1 = (s32[8,1,128]{2,1,0:T(1,128)S(1)}, s32[8,1,128]{2,1,0:T(1,128)S(1)}, u32[]{:S(2)}, u32[]{:S(2)}) collective-permute-start(s32[8,1,128]{2,1,0:T(1,128)S(1)} %bitcast.8), channel_id=1, source_target_pairs={{0,2},{1,3},{2,0},{3,1},{4,6},{5,7},{6,4},{7,5},{8,10},{9,11},{10,... | collective-permute-start | bytes 12296 | tf_op jit(solution)/shard_map/ppermute | solution.py:353
  51.6 4.4 %collective-permute-start = (s32[8,1,128]{2,1,0:T(1,128)S(1)}, s32[8,1,128]{2,1,0:T(1,128)S(1)}, u32[]{:S(2)}, u32[]{:S(2)}) collective-permute-start(s32[8,1,128]{2,1,0:T(1,128)S(1)} %bitcast.9), channel_id=1, source_target_pairs={{0,1},{1,0},{2,3},{3,2},{4,5},{5,4},{6,7},{7,6},{8,9},{9,8},{10,11... | collective-permute-start | bytes 12296 | tf_op jit(solution)/shard_map/ppermute | solution.py:353
  97.6 39.9 %copy-start.1 = (bf16[1024,512]{1,0:T(8,128)(2,1)S(1)}, bf16[1024,512]{1,0:T(8,128)(2,1)}, u32[]{:S(2)}) copy-start(bf16[1024,512]{1,0:T(8,128)(2,1)} %attend.3) | copy-start | bytes 3145732
Sparse Core Ops, SparseCore 0:
  9.7 81.1 all-gather.2
where the time goes:
time: 331 us; the launch traced here: 330 us
  Pallas kernels  281 us (85%)
  between operations  14.1 us (4%)
  local copies, waits for them, and re-layouts  13.2 us (4%)
  other arithmetic  9.16 us (3%)
  waiting for transfers between devices  8.51 us (3%)
  starting transfers between devices  4.34 us (1%)
    pallas_call x1, Pallas kernels, local_block(): pl.pallas_call(functools.partial(out_kernel, n_tp, n_cp), out_shape=jax.S...  175 us
    pallas_call x2, Pallas kernels, attend(): pl.pallas_call(functools.partial(attn_kernel, head, n_kv), grid=(n_q,), o...  79.7 us
    pallas_call x1, Pallas kernels, local_block(): pl.pallas_call(q_kernel, grid=(rows // rb,), out_shape=jax.ShapeDtypeStru...  14.9 us
    pallas_call x1, Pallas kernels, local_block(): pl.pallas_call(kv_kernel, grid=(rows // rb,), out_shape=(jax.ShapeDtypeSt...  11.2 us
    ppermute x1, waiting for transfers between devices, local_block(): kv_chip = lax.ppermute(kv, 'cp', swap_chip)  8.48 us
    unnamed x9, local copies, waits for them, and re-layouts  7.9 us
  transfers between devices with their start and end apart: 7, of which 1 were waited for; matrix products, arithmetic and copies ran while one was open for 4% of the time, Pallas kernels for 32%

commit v1 on v0

v1 whole, which is shorter than its diff:
```python
import functools
import math

import jax
import jax.numpy as jnp
from jax import lax
from jax.experimental import pallas as pl
from jax.experimental.pallas import tpu as pltpu
from jax.sharding import PartitionSpec as P

HEAD = 128
THETA = 1000000
EPS = 1e-5
NEG_BIG = -1e30
KB = 128
GROUP = 4
WIDE = 8
PARTS = 1
AHEAD = 2
QB = 128


def rope_tables(tok_pos):
    inv_freq = 1.0 / (THETA ** (jnp.arange(0, HEAD, 2, dtype=jnp.float32) / HEAD))
    inv_freq = jnp.concatenate([inv_freq, inv_freq])
    sign = jnp.where(jnp.arange(HEAD) < HEAD // 2, -1.0, 1.0).astype(jnp.float32)
    angles = tok_pos.astype(jnp.float32)[:, None] * inv_freq[None, :]
    return jnp.cos(angles), jnp.sin(angles) * sign[None, :]


def rotate(x_f32, cos_tab, sin_tab):
    x = x_f32.astype(jnp.bfloat16).astype(jnp.float32)
    return (x * cos_tab + pltpu.roll(x, HEAD // 2, 1) * sin_tab).astype(jnp.bfloat16)


def kv_kernel(x_ref, gain_ref, wk_ref, wv_ref, cos_ref, sin_ref, normed_ref, kv_ref):
    x = x_ref[...].astype(jnp.float32)
    var = jnp.mean(x * x, axis=-1, keepdims=True)
    normed = (x * lax.rsqrt(var + EPS) * gain_ref[...]).astype(jnp.bfloat16)
    normed_ref[...] = normed
    n_k = wk_ref.shape[1]
    k = jnp.dot(normed, wk_ref[...], preferred_element_type=jnp.float32)
    v = jnp.dot(normed, wv_ref[...], preferred_element_type=jnp.float32)
    for h in range(n_k // HEAD):
        cols = slice(h * HEAD, (h + 1) * HEAD)
        kv_ref[:, cols] = rotate(k[:, cols], cos_ref[...], sin_ref[...])
    kv_ref[:, n_k:] = v.astype(jnp.bfloat16)


def q_kernel(normed_ref, wq_ref, cos_ref, sin_ref, q_ref):
    for c in range(0, wq_ref.shape[1], 2 * HEAD):
        q = jnp.dot(normed_ref[...], wq_ref[:, c:c + 2 * HEAD], preferred_element_type=jnp.float32)
        for h in range(2):
            q_ref[:, c + h * HEAD:c + (h + 1) * HEAD] = rotate(q[:, h * HEAD:(h + 1) * HEAD], cos_ref[...], sin_ref[...])


def attn_kernel(first, kmin_ref, kmax_ref, qmin_ref, qmax_ref, q_ref, posq_ref, posk_ref, kv0, kv1, kv2, kv3, o_ref,
                kv_s, q_s, pq_s, m_s, l_s, acc_s, full_l, part_l, sems):
    step = pl.program_id(0)
    rows = kv0.shape[0]
    n_blocks = kmin_ref.shape[0]
    n_kv = kv0.shape[1] // (2 * HEAD)
    n_heads = q_ref.shape[1] // HEAD
    per_kv = n_heads // n_kv

    @pl.when(step == 0)
    def _():
        copies = [pltpu.make_async_copy(src, kv_s.at[pl.ds(i * rows, rows), :], sems.at[i]) for i, src in enumerate((kv0, kv1, kv2, kv3))]
        for c in copies:
            c.start()
        for c in copies:
            c.wait()

    q_lo = qmin_ref[first + step]
    q_hi = qmax_ref[first + step]

    def classify(j, counts):
        n_full, n_part = counts
        lo, hi = kmin_ref[j], kmax_ref[j]
        is_full = hi <= q_lo
        is_part = jnp.logical_and(lo <= q_hi, jnp.logical_not(is_full))

        @pl.when(is_full)
        def _():
            full_l[n_full] = j

        @pl.when(is_part)
        def _():
            part_l[n_part] = j

        return n_full + is_full.astype(jnp.int32), n_part + is_part.astype(jnp.int32)

    n_full, n_part = lax.fori_loop(0, n_blocks, classify, (0, 0))
    n_groups = n_full // WIDE

    def move(i, n_part):
        part_l[n_part] = full_l[n_groups * WIDE + i]
        return n_part + 1

    n_part = lax.fori_loop(0, n_full - n_groups * WIDE, move, n_part)
    n_mgroups = (n_part + GROUP - 1) // GROUP

    def pad(i, _):
        part_l[n_part + i] = 0
        return 0

    lax.fori_loop(0, n_mgroups * GROUP - n_part, pad, 0)

    for h in range(n_heads):
        q_s[h * QB:(h + 1) * QB, :] = q_ref[:, h * HEAD:(h + 1) * HEAD]
    part_rows = per_kv * QB // PARTS
    for h in range(part_rows // QB):
        pq_s[h * QB:(h + 1) * QB, :] = jnp.broadcast_to(posq_ref[...], (QB, HEAD))
    m_s[...] = jnp.full_like(m_s, NEG_BIG)
    l_s[...] = jnp.zeros_like(l_s)
    acc_s[...] = jnp.zeros_like(acc_s)

    scale = HEAD ** -0.5 * math.log2(math.e)

    def absorb(blocks, pos_rows):
        def gather(c0):
            return jnp.concatenate([kv_s[pl.ds(pl.multiple_of(b * KB, KB), KB), c0:c0 + HEAD] for b in blocks], axis=0)

        ks = [gather(g * HEAD) for g in range(n_kv)]
        vs = [gather((n_kv + g) * HEAD) for g in range(n_kv)]
        n = len(blocks)
        chains = [(g, slice((g * PARTS + i) * part_rows, (g * PARTS + i + 1) * part_rows)) for i in range(PARTS) for g in range(n_kv)]

        def scores(g, sl):
            return lax.dot_general(q_s[sl, :], ks[g], (((1,), (1,)), ((), ())), preferred_element_type=jnp.float32)

        ahead = [scores(*c) for c in chains[:AHEAD]]
        for i, (g, sl) in enumerate(chains):
            s = ahead[i]
            if i + AHEAD < len(chains):
                ahead.append(scores(*chains[i + AHEAD]))
            cols = [s[:, c * KB:(c + 1) * KB] * scale for c in range(n)]
            if pos_rows is not None:
                cols = [jnp.where(pr <= pq_s[...], c, NEG_BIG) for pr, c in zip(pos_rows, cols)]
            top = cols[0]
            for c in cols[1:]:
                top = jnp.maximum(top, c)
            m_old = m_s[sl, :]
            m_new = jnp.maximum(m_old, jnp.max(top, axis=-1, keepdims=True))
            alpha = jnp.exp2(m_old - m_new)
            p = [jnp.exp2(c - m_new) for c in cols]
            total = p[0]
            for c in p[1:]:
                total = total + c
            l_s[sl, :] = l_s[sl, :] * alpha + total
            pv = jnp.dot(jnp.concatenate([c.astype(jnp.bfloat16) for c in p], axis=1), vs[g], preferred_element_type=jnp.float32)
            acc_s[sl, :] = acc_s[sl, :] * alpha + pv
            m_s[sl, :] = m_new

    def full_step(i, _):
        absorb([full_l[i * WIDE + c] for c in range(WIDE)], None)
        return 0

    lax.fori_loop(0, n_groups, full_step, 0)

    def part_step(i, _):
        blocks = [part_l[i * GROUP + c] for c in range(GROUP)]
        absorb(blocks, [posk_ref[b] + jnp.where(i * GROUP + c < n_part, 0, 1 << 30) for c, b in enumerate(blocks)])
        return 0

    lax.fori_loop(0, n_mgroups, part_step, 0)

    for h in range(n_heads):
        sl = slice(h * QB, (h + 1) * QB)
        o_ref[:, h * HEAD:(h + 1) * HEAD] = (acc_s[sl, :] / jnp.sum(l_s[sl, :], axis=-1, keepdims=True)).astype(jnp.bfloat16)


TILE = 512
N_CHUNK = 4


def out_kernel(n_tp, n_cp, oa_hbm, ob_hbm, la_hbm, w_hbm, z_hbm, x_hbm, out_hbm, o_buf, w_buf, acc, w_t, x_t, y_t,
               o_send, o_recv, w_send, w_recv, w_local, ld_sem, st_sem, own_sem):
    mesh_id = pl.DeviceIdType.MESH
    tp, dp, cp = lax.axis_index("tp"), lax.axis_index("dp"), lax.axis_index("cp")
    core, chip = cp % 2, cp // 2
    cp_y = cp + 2 - 4 * chip
    to_right, to_left = {"tp": (tp + 1) % n_tp}, {"tp": (tp + n_tp - 1) % n_tp}
    to_x, to_y, to_p = {"dp": 1 - dp}, {"cp": cp_y}, {"cp": cp + 1 - 2 * core}
    p_me, p_x, p_y, p_d = dp * n_cp + cp, (1 - dp) * n_cp + cp, dp * n_cp + cp_y, (1 - dp) * n_cp + cp_y
    sl = z_hbm.shape[1]
    n_rows, width = acc.shape
    half = n_rows // 2
    ch = n_rows // N_CHUNK
    n_tile = width // TILE
    last = n_tp - 1

    barrier = pltpu.get_barrier_semaphore()
    for peer in (to_right, to_left, to_x, to_y, to_p):
        pl.semaphore_signal(barrier, inc=1, device_id=peer, device_id_type=mesh_id)
    pl.semaphore_wait(barrier, 5)

    def o_copy(s, c):
        at = pl.ds(c * ch, ch)
        if s == 0:
            src = ob_hbm.at[pl.ds(c * ch - half, ch), :]
        elif s == 1 and c * ch < half:
            src = la_hbm.at[at, :]
        else:
            src = o_buf.at[s, at, :]
        return pltpu.make_async_remote_copy(src_ref=src, dst_ref=o_buf.at[s + 1, at, :], send_sem=o_send.at[s, c],
                                            recv_sem=o_recv.at[s, c], device_id=to_right, device_id_type=mesh_id)

    def rows(p, first=0, n=None):
        return pl.ds(pl.multiple_of(p * sl + first, sl // 2), sl if n is None else n)

    def w_copy(k, kind):
        hs = sl // 2
        own = z_hbm.at[(tp + n_tp - k - 1) % n_tp]
        idx, peer, where = {
            "own_x": (0, to_x, rows(p_me)), "own_y": (1, to_y, rows(p_me)), "own_p": (2, to_p, rows(p_me)),
            "dx": (3, to_x, rows(p_y, hs, hs)), "dy": (4, to_y, rows(p_x, 0, hs)),
            "px": (5, to_p, rows(p_x)), "py": (6, to_p, rows(p_y)),
            "pd0": (7, to_p, rows(p_d, 0, hs)), "pd1": (8, to_p, rows(p_d, hs, hs)),
        }[kind]
        src = own if idx < 3 else w_buf.at[k, where, :]
        return pltpu.make_async_remote_copy(src_ref=src, dst_ref=w_buf.at[k, where, :], send_sem=w_send.at[k, idx],
                                            recv_sem=w_recv.at[k, idx], device_id=peer, device_id_type=mesh_id)

    def w_own_local(k):
        return pltpu.make_async_copy(z_hbm.at[(tp + n_tp - k - 1) % n_tp], w_buf.at[k, rows(p_me), :], w_local.at[k])

    def start_own(k):
        for kind in ("own_x", "own_y", "own_p"):
            w_copy(k, kind).start()
        w_own_local(k).start()

    def pass_on(k):
        w_copy(k, "own_x").wait_recv()
        w_copy(k, "own_y").wait_recv()
        for kind in ("dx", "dy", "px", "py"):
            w_copy(k, kind).start()

    def pass_diag(k):
        w_copy(k, "dy").wait_recv()
        w_copy(k, "pd0").start()
        w_copy(k, "dx").wait_recv()
        w_copy(k, "pd1").start()

    def complete(k):
        w_own_local(k).wait()
        for kind in ("own_p", "px", "py", "pd0", "pd1"):
            w_copy(k, kind).wait_recv()

    def arrive(s, c):
        o_copy(s - 1, c).wait_recv()
        if s < last:
            o_copy(s, c).start()

    def tile_cols(t):
        return pl.ds(pl.multiple_of(t * TILE, TILE), TILE)

    def accum(s, r0, r1):
        def body(t, _):
            cols = tile_cols(t)
            acc[r0:r1, cols] += jnp.dot(o_buf[s, r0:r1, :], w_buf[s - 1, :, cols], preferred_element_type=jnp.float32)
            return 0

        lax.fori_loop(0, n_tile, body, 0)

    for c in (0, 1):
        o_copy(1, c).start()
    for c in (2, 3):
        o_copy(0, c).start()
    start_own(0)
    own = [pltpu.make_async_copy(oa_hbm, o_buf.at[0, pl.ds(0, half), :], own_sem.at[0]),
           pltpu.make_async_copy(ob_hbm, o_buf.at[0, pl.ds(half, half), :], own_sem.at[1]),
           pltpu.make_async_copy(la_hbm, o_buf.at[1, pl.ds(0, half), :], own_sem.at[2])]
    for d in own:
        d.start()

    def loads(t, slot):
        cols = tile_cols(t)
        return (pltpu.make_async_copy(w_hbm.at[:, cols], w_t.at[slot], ld_sem.at[slot, 0]),
                pltpu.make_async_copy(x_hbm.at[:, cols], x_t.at[slot], ld_sem.at[slot, 1]))

    for d in loads(0, 0):
        d.start()
    for d in own:
        d.wait()

    def first(t, _):
        slot = t % 2

        @pl.when(t + 1 < n_tile)
        def _():
            for d in loads(t + 1, (t + 1) % 2):
                d.start()

        for d in loads(t, slot):
            d.wait()
        acc[:, tile_cols(t)] = x_t[slot].astype(jnp.float32) + jnp.dot(o_buf[0], w_t[slot], preferred_element_type=jnp.float32)
        return 0

    lax.fori_loop(0, n_tile, first, 0)

    def store(r0, t, slot):
        return pltpu.make_async_copy(y_t.at[slot], out_hbm.at[pl.ds(r0, ch), tile_cols(t)], st_sem.at[slot])

    def finish(c):
        r0 = c * ch

        def body(t, _):
            slot = t % 2

            @pl.when(t >= 2)
            def _():
                store(r0, t - 2, slot).wait()

            cols = tile_cols(t)
            y = acc[r0:r0 + ch, cols] + jnp.dot(o_buf[last, r0:r0 + ch, :], w_buf[last - 1, :, cols], preferred_element_type=jnp.float32)
            y_t[slot] = y.astype(jnp.bfloat16)
            store(r0, t, slot).start()
            return 0

        lax.fori_loop(0, n_tile, body, 0)
        store(r0, n_tile - 2, n_tile % 2).wait()
        store(r0, n_tile - 1, (n_tile - 1) % 2).wait()

    pass_on(0)
    start_own(1)
    arrive(2, 0)
    arrive(2, 1)
    pass_diag(0)
    arrive(1, 2)
    complete(0)
    accum(1, 0, half)
    arrive(1, 3)
    accum(1, half, n_rows)
    pass_on(1)
    start_own(2)
    arrive(3, 0)
    pass_diag(1)
    arrive(3, 1)
    complete(1)
    accum(2, 0, half)
    arrive(2, 2)
    pass_on(2)
    arrive(2, 3)
    accum(2, half, n_rows)
    pass_diag(2)
    complete(2)
    finish(0)
    finish(1)
    arrive(3, 2)
    finish(2)
    arrive(3, 3)
    finish(3)

    for s in range(last):
        for c in range(N_CHUNK):
            if s > 0 or c >= 2:
                o_copy(s, c).wait_send()
        for kind in ("own_x", "own_y", "own_p", "dx", "dy", "px", "py", "pd0", "pd1"):
            w_copy(s, kind).wait_send()


def solution(mesh):
    n_tp, n_cp, n_dp = mesh.shape["tp"], mesh.shape["cp"], mesh.shape["dp"]
    plane = n_dp * n_cp
    ring = [(i, (i + 1) % n_tp) for i in range(n_tp)]
    swap_core = [(i, i ^ 1) for i in range(n_cp)]
    swap_chip = [(i, i ^ 2) for i in range(n_cp)]

    def local_block(hidden, tok_pos, norm_gain, w_query, w_key, w_value, w_out):
        rows, width = hidden.shape
        q_cols, k_cols = w_query.shape[1], w_key.shape[1]
        n_kv = k_cols // HEAD
        plane_idx = lax.axis_index("dp") * n_cp + lax.axis_index("cp")

        slice_rows = w_out.shape[0] // plane
        own_slice = lax.dynamic_slice_in_dim(w_out, plane_idx * slice_rows, slice_rows, axis=0)
        z_slices = lax.all_gather(own_slice, "tp", axis=0, tiled=False)

        cos_tab, sin_tab = rope_tables(tok_pos)
        rb = 256
        row_blk = lambda cols: pl.BlockSpec((rb, cols), lambda i: (i, 0))
        whole = lambda r, c: pl.BlockSpec((r, c), lambda i: (0, 0))
        normed, kv = pl.pallas_call(
            kv_kernel,
            grid=(rows // rb,),
            out_shape=(jax.ShapeDtypeStruct((rows, width), jnp.bfloat16), jax.ShapeDtypeStruct((rows, 2 * k_cols), jnp.bfloat16)),
            in_specs=[row_blk(width), whole(1, width), whole(width, k_cols), whole(width, k_cols), row_blk(HEAD), row_blk(HEAD)],
            out_specs=(row_blk(width), row_blk(2 * k_cols)),
            cost_estimate=pl.CostEstimate(flops=4 * rows * width * k_cols, bytes_accessed=24 << 20, transcendentals=0),
            name="norm_kv",
        )(hidden, norm_gain.reshape(1, width), w_key, w_value, cos_tab, sin_tab)

        pos_row = tok_pos.reshape(rows // KB, 1, KB)
        kv_core = lax.ppermute(kv, "cp", swap_core)
        kv_chip = lax.ppermute(kv, "cp", swap_chip)
        swap_diag = [(i, i ^ 3) for i in range(n_cp)]
        pos_rel = jnp.concatenate([pos_row] + [lax.ppermute(pos_row, "cp", pairs) for pairs in (swap_core, swap_chip, swap_diag)], axis=0)

        q_rot = pl.pallas_call(
            q_kernel,
            grid=(rows // rb,),
            out_shape=jax.ShapeDtypeStruct((rows, q_cols), jnp.bfloat16),
            in_specs=[row_blk(width), whole(width, q_cols), row_blk(HEAD), row_blk(HEAD)],
            out_specs=row_blk(q_cols),
            cost_estimate=pl.CostEstimate(flops=2 * rows * width * q_cols, bytes_accessed=20 << 20, transcendentals=0),
            name="q_rope",
        )(normed, w_query, cos_tab, sin_tab)

        kv_chip, q_rot = lax.optimization_barrier((kv_chip, q_rot))
        kv_diag = lax.ppermute(kv_chip, "cp", swap_core)

        kmin, kmax = jnp.min(pos_rel, axis=(1, 2)), jnp.max(pos_rel, axis=(1, 2))
        n_q = rows // QB
        qpos = tok_pos.reshape(n_q, QB)
        qmin, qmax = jnp.min(qpos, axis=1), jnp.max(qpos, axis=1)
        pos_col = tok_pos.reshape(rows, 1)
        smem = pl.BlockSpec(memory_space=pltpu.SMEM)
        anym = pl.BlockSpec(memory_space=pl.ANY)

        def attend(part, n_parts):
            steps = n_q // n_parts
            first = part * steps
            n_rows = (q_cols // HEAD) * QB
            blocks_max = n_cp * rows // KB
            return pl.pallas_call(
                functools.partial(attn_kernel, first),
                grid=(steps,),
                out_shape=jax.ShapeDtypeStruct((rows // n_parts, q_cols), jnp.bfloat16),
                in_specs=[smem] * 4 + [pl.BlockSpec((QB, q_cols), lambda i: (first + i, 0)), pl.BlockSpec((QB, 1), lambda i: (first + i, 0)),
                                       pl.BlockSpec(pos_rel.shape, lambda i: (0, 0, 0))] + [anym] * 4,
                out_specs=pl.BlockSpec((QB, q_cols), lambda i: (i, 0)),
                scratch_shapes=[
                    pltpu.VMEM((n_cp * rows, 2 * k_cols), jnp.bfloat16),
                    pltpu.VMEM((n_rows, HEAD), jnp.bfloat16),
                    pltpu.VMEM((n_rows // n_kv // PARTS, HEAD), jnp.int32),
                    pltpu.VMEM((n_rows, HEAD), jnp.float32),
                    pltpu.VMEM((n_rows, HEAD), jnp.float32),
                    pltpu.VMEM((n_rows, HEAD), jnp.float32),
                    pltpu.SMEM((blocks_max + WIDE,), jnp.int32),
                    pltpu.SMEM((blocks_max + WIDE + GROUP,), jnp.int32),
                    pltpu.SemaphoreType.DMA((4,)),
                ],
                cost_estimate=pl.CostEstimate(flops=4 * rows // n_parts * n_cp * rows * q_cols, bytes_accessed=8 << 20, transcendentals=0),
                name="attend",
            )(kmin, kmax, qmin, qmax, q_rot, pos_col, pos_rel, kv, kv_core, kv_chip, kv_diag)

        o_a = attend(0, 2)
        left_a = lax.ppermute(o_a, "tp", ring)
        o_b = attend(1, 2)
        hidden_out = pl.pallas_call(
            functools.partial(out_kernel, n_tp, n_cp),
            out_shape=jax.ShapeDtypeStruct((rows, width), jnp.bfloat16),
            in_specs=[anym] * 6,
            out_specs=anym,
            scratch_shapes=[
                pltpu.VMEM((n_tp, rows, q_cols), jnp.bfloat16),
                pltpu.VMEM((n_tp - 1, q_cols, width), jnp.bfloat16),
                pltpu.VMEM((rows, width), jnp.float32),
                pltpu.VMEM((2, q_cols, TILE), jnp.bfloat16),
                pltpu.VMEM((2, rows, TILE), jnp.bfloat16),
                pltpu.VMEM((2, rows // N_CHUNK, TILE), jnp.bfloat16),
                pltpu.SemaphoreType.DMA((n_tp - 1, N_CHUNK)),
                pltpu.SemaphoreType.DMA((n_tp - 1, N_CHUNK)),
                pltpu.SemaphoreType.DMA((n_tp - 1, 9)),
                pltpu.SemaphoreType.DMA((n_tp - 1, 9)),
                pltpu.SemaphoreType.DMA((n_tp - 1,)),
                pltpu.SemaphoreType.DMA((2, 2)),
                pltpu.SemaphoreType.DMA((2,)),
                pltpu.SemaphoreType.DMA((3,)),
            ],
            compiler_params=pltpu.CompilerParams(collective_id=0, has_side_effects=True, vmem_limit_bytes=63 << 20),
            cost_estimate=pl.CostEstimate(flops=2 * n_tp * rows * q_cols * width, bytes_accessed=48 << 20, transcendentals=0),
            name="out_gather",
        )(o_a, o_b, left_a, w_out, z_slices, hidden)
        k_cache = kv[:, :k_cols].reshape(rows, n_kv, HEAD)
        v_cache = kv[:, k_cols:].reshape(rows, n_kv, HEAD)
        return hidden_out, k_cache, v_cache

    row_spec = P(("dp", "cp"), None)
    cache_spec = P(("dp", "cp"), "tp", None)
    return jax.shard_map(local_block, mesh=mesh, in_specs=(row_spec, P(("dp", "cp")), P(None), P(None, "tp"), P(None, "tp"), P(None, "tp"), P("tp", None)), out_specs=(row_spec, cache_spec, cache_spec), check_vma=False)
```

time: 331 us -> 262 us (0.79)
  the two profiles are of different devices: /device:TPU:5 before, /device:TPU:1 now
where the time goes in v1:
time: 262 us; the launch traced here: 261 us
  Pallas kernels  197 us (75%)
  waiting for transfers between devices  22.2 us (8%)
  local copies, waits for them, and re-layouts  14.1 us (5%)
  between operations  14.1 us (5%)
  starting transfers between devices  7.87 us (3%)
  other arithmetic  6.32 us (2%)
    pallas_call x1, Pallas kernels, local_block(): pl.pallas_call(functools.partial(out_kernel, n_tp, n_cp), out_shape=jax.S...  135 us
    pallas_call x2, Pallas kernels, attend(): pl.pallas_call(functools.partial(attn_kernel, first), grid=(steps,), out_...  36.1 us
    pallas_call x1, Pallas kernels, local_block(): pl.pallas_call(q_kernel, grid=(rows // rb,), out_shape=jax.ShapeDtypeStru...  14.8 us
    ppermute x1, waiting for transfers between devices, local_block(): left_a = lax.ppermute(o_a, 'tp', ring)  14.6 us
    pallas_call x1, Pallas kernels, local_block(): pl.pallas_call(kv_kernel, grid=(rows // rb,), out_shape=(jax.ShapeDtypeSt...  11.2 us
    unnamed x9, local copies, waits for them, and re-layouts  8.87 us
    ppermute x1, waiting for transfers between devices, local_block(): kv_chip = lax.ppermute(kv, 'cp', swap_chip)  7.17 us
  transfers between devices with their start and end apart: 8, of which 3 were waited for; matrix products, arithmetic and copies ran while one was open for 4% of the time, Pallas kernels for 24%

profile of v1, /device:TPU:1, one launch (start us, length us, event | category | flops | bytes accessed | tf_op | source)
XLA Modules:
  0.0 261.3 jit_solution(4785296279691095421)
XLA Ops:
  7.2 2.3 constant_dynamic-slice_fusion
  9.5 0.7 convert_element_type.3
  10.3 3.0 %fusion = (f32[1024,128]{1,0:T(8,128)}, f32[1024,128]{1,0:T(8,128)}) fusion(f32[128]{0:T(128)S(1)} %get-tuple-element.20, f32[128]{0:T(128)S(1)} %get-tuple-element.21, f32[1024]{0:T(1024)S(1)} %convert_element_type.3), kind=kLoop, calls=%fused_computation.2 | loop fusion | flops 262144 | bytes 1053696 | tf_op jit(solution)/shard_map/mul | solution.py:28
  13.4 11.2 %norm_kv.1 = (bf16[1024,4096]{1,0:T(8,128)(2,1)}, bf16[1024,512]{1,0:T(8,128)(2,1)}) custom-call(bf16[1024,4096]{1,0:T(8,128)(2,1)} %x_hbm.1, f32[1,4096]{1,0:T(1,128)} %bitcast.13, bf16[4096,256]{1,0:T(8,128)(2,1)} %wk_ref.1, bf16[4096,256]{1,0:T(8,128)(2,1)} %wv_ref.1, f32[1024,128]{1,0:T(8,128)} %get-tuple-element.19.cos_ref, ...), custom_call_target="tpu_custom_call" | custom-call | flops 4294967296 | bytes 25165824 | tf_op jit(solution)/shard_map/norm_kv/pallas_call | solution.py:384
  24.6 2.1 collective-permute-start.3
  26.7 1.0 collective-permute-start.4
  27.6 14.8 %q_rope.1.q_ref = bf16[1024,1024]{1,0:T(8,128)(2,1)} custom-call(bf16[1024,4096]{1,0:T(8,128)(2,1)} %get-tuple-element.8.normed_ref, bf16[4096,1024]{1,0:T(8,128)(2,1)} %wq_ref.1, f32[1024,128]{1,0:T(8,128)} %get-tuple-element.19.cos_ref, f32[1024,128]{1,0:T(8,128)} %get-tuple-element.18.sin_ref), custom_call_target="tpu_custom_call" | custom-call | flops 8589934592 | bytes 20971520 | tf_op jit(solution)/shard_map/q_rope/pallas_call | solution.py:400
  42.5 7.2 %collective-permute-done.3.kv2 = bf16[1024,512]{1,0:T(8,128)(2,1)S(1)} collective-permute-done((bf16[1024,512]{1,0:T(8,128)(2,1)}, bf16[1024,512]{1,0:T(8,128)(2,1)S(1)}, u32[]{:S(2)}, u32[]{:S(2)}) %collective-permute-start.3) | collective-permute-done | bytes 1048608 | tf_op jit(solution)/shard_map/ppermute | solution.py:396
  49.6 1.1 collective-permute-start.5
  50.8 1.4 collective-permute-start.2
  52.2 0.7 collective-permute-start
  52.9 0.7 bitcast_reduce_fusion
  53.6 1.0 copy.12.posq_ref
  54.6 0.4 collective-permute-done.1
  55.1 1.8 fusion.1
  56.9 1.0 copy-done.3
  57.9 15.8 %attend.2.oa_hbm = bf16[512,1024]{1,0:T(8,128)(2,1)} custom-call(s32[32]{0:T(128)} %get-tuple-element.12.kmin_ref, s32[32]{0:T(128)} %get-tuple-element.11.kmax_ref, s32[8]{0:T(128)} %get-tuple-element.14.qmin_ref, s32[8]{0:T(128)} %get-tuple-element.13.qmax_ref, bf16[1024,1024]{1,0:T(8,128)(2,1)} %q_rope.1.q_ref, s32[1024,1]{1,0:T(8,128)} %copy.12.posq_ref, ...), custom_call_target="tpu_custom_call" | custom-call | flops 8589934592 | bytes 8388608 | tf_op jit(solution)/shard_map/attend/pallas_call | solution.py:426
  73.6 1.5 collective-permute-start.6
  75.2 0.9 reshape.36
  76.2 0.9 reshape.35
  77.1 20.3 %attend.3.ob_hbm = bf16[512,1024]{1,0:T(8,128)(2,1)} custom-call(s32[32]{0:T(128)} %get-tuple-element.12.kmin_ref, s32[32]{0:T(128)} %get-tuple-element.11.kmax_ref, s32[8]{0:T(128)} %get-tuple-element.14.qmin_ref, s32[8]{0:T(128)} %get-tuple-element.13.qmax_ref, bf16[1024,1024]{1,0:T(8,128)(2,1)} %q_rope.1.q_ref, s32[1024,1]{1,0:T(8,128)} %copy.12.posq_ref, ...), custom_call_target="tpu_custom_call" | custom-call | flops 8589934592 | bytes 8388608 | tf_op jit(solution)/shard_map/attend/pallas_call | solution.py:426
  97.4 14.6 %collective-permute-done.6.la_hbm = bf16[512,1024]{1,0:T(8,128)(2,1)} collective-permute-done((bf16[512,1024]{1,0:T(8,128)(2,1)}, bf16[512,1024]{1,0:T(8,128)(2,1)}, u32[]{:S(2)}, u32[]{:S(2)}) %collective-permute-start.6) | collective-permute-done | bytes 1048608 | tf_op jit(solution)/shard_map/ppermute | solution.py:449
  112.0 134.5 %out_gather.1 = bf16[1024,4096]{1,0:T(8,128)(2,1)} custom-call(bf16[512,1024]{1,0:T(8,128)(2,1)} %attend.2.oa_hbm, bf16[512,1024]{1,0:T(8,128)(2,1)} %attend.3.ob_hbm, bf16[512,1024]{1,0:T(8,128)(2,1)} %collective-permute-done.6.la_hbm, bf16[1024,4096]{1,0:T(8,128)(2,1)} %w_hbm.1, bf16[4,128,4096]{2,1,0:T(8,128)(2,1)} %bitcast.12, bf16[1024,4096]{1,0:T(8,128)(2,1)} %x_hbm.1), custom_call_target="tpu_custom_call" | custom-call | flops 34359738368 | bytes 50331648 | tf_op jit(solution)/shard_map/out_gather/pallas_call | solution.py:451
  246.6 7.9 %copy.15 = bf16[1024,4096]{1,0:T(8,128)(2,1)} copy(bf16[1024,4096]{1,0:T(8,128)(2,1)} %out_gather.1) | data formatting | bytes 16777216
  (18 shorter events, 0.3 us)
Async XLA Ops:
  7.2 104.9 %all-gather.3.cloned.1.call-start = ((), (), s32[]{:S(2)}) async-start(), calls=%async_computation | async-start | bytes 5242880 | tf_op jit(solution)/shard_map/all_gather | solution.py:378
  24.6 25.0 %collective-permute-start.3 = (bf16[1024,512]{1,0:T(8,128)(2,1)}, bf16[1024,512]{1,0:T(8,128)(2,1)S(1)}, u32[]{:S(2)}, u32[]{:S(2)}) collective-permute-start(bf16[1024,512]{1,0:T(8,128)(2,1)} %get-tuple-element.7.kv0), channel_id=1, source_target_pairs={{0,2},{1,3},{2,0},{3,1},{4,6},{5,7},{6,4},{7,5},{8,10},{9,11},{10,... | collective-permute-start | bytes 3145736 | tf_op jit(solution)/shard_map/ppermute | solution.py:396
  26.7 30.2 %collective-permute-start.4 = (bf16[1024,512]{1,0:T(8,128)(2,1)}, bf16[1024,512]{1,0:T(8,128)(2,1)S(1)}, u32[]{:S(2)}, u32[]{:S(2)}) collective-permute-start(bf16[1024,512]{1,0:T(8,128)(2,1)} %get-tuple-element.7.kv0), channel_id=1, source_target_pairs={{0,1},{1,0},{2,3},{3,2},{4,5},{5,4},{6,7},{7,6},{8,9},{9,8},{10,11... | collective-permute-start | bytes 3145736 | tf_op jit(solution)/shard_map/ppermute | solution.py:395
  27.6 23.2 %copy-start.1 = (s32[1024]{0:T(1024)S(1)}, s32[1024]{0:T(1024)}, u32[]{:S(2)}) copy-start(s32[1024]{0:T(1024)} %param.8) | copy-start | bytes 12292
  49.6 8.2 %copy-start.2 = (bf16[1024,512]{1,0:T(8,128)(2,1)}, bf16[1024,512]{1,0:T(8,128)(2,1)S(1)}, u32[]{:S(2)}) copy-start(bf16[1024,512]{1,0:T(8,128)(2,1)S(1)} %collective-permute-done.3.kv2) | copy-start | bytes 3145732
  49.6 7.2 %collective-permute-start.5 = (bf16[1024,512]{1,0:T(8,128)(2,1)S(1)}, bf16[1024,512]{1,0:T(8,128)(2,1)}, u32[]{:S(2)}, u32[]{:S(2)}) collective-permute-start(bf16[1024,512]{1,0:T(8,128)(2,1)S(1)} %collective-permute-done.3.kv2), channel_id=1, source_target_pairs={{0,1},{1,0},{2,3},{3,2},{4,5},{5,4},{6,7},{7,6},{8,9},{9,8},{10,11... | collective-permute-start | bytes 3145736 | tf_op jit(solution)/shard_map/ppermute | solution.py:411
  50.8 3.9 %collective-permute-start.2 = (s32[8,1,128]{2,1,0:T(1,128)S(1)}, s32[8,1,128]{2,1,0:T(1,128)S(1)}, u32[]{:S(2)}, u32[]{:S(2)}) collective-permute-start(s32[8,1,128]{2,1,0:T(1,128)S(1)} %bitcast.7), channel_id=1, source_target_pairs={{0,3},{1,2},{2,1},{3,0},{4,7},{5,6},{6,5},{7,4},{8,11},{9,10},{10,... | collective-permute-start | bytes 12296 | tf_op jit(solution)/shard_map/ppermute | solution.py:398
  52.2 2.9 %collective-permute-start.1 = (s32[8,1,128]{2,1,0:T(1,128)S(1)}, s32[8,1,128]{2,1,0:T(1,128)S(1)}, u32[]{:S(2)}, u32[]{:S(2)}) collective-permute-start(s32[8,1,128]{2,1,0:T(1,128)S(1)} %bitcast.8), channel_id=1, source_target_pairs={{0,2},{1,3},{2,0},{3,1},{4,6},{5,7},{6,4},{7,5},{8,10},{9,11},{10,... | collective-permute-start | bytes 12296 | tf_op jit(solution)/shard_map/ppermute | solution.py:398
  52.2 2.8 %collective-permute-start = (s32[8,1,128]{2,1,0:T(1,128)S(1)}, s32[8,1,128]{2,1,0:T(1,128)S(1)}, u32[]{:S(2)}, u32[]{:S(2)}) collective-permute-start(s32[8,1,128]{2,1,0:T(1,128)S(1)} %bitcast.9), channel_id=1, source_target_pairs={{0,1},{1,0},{2,3},{3,2},{4,5},{5,4},{6,7},{7,6},{8,9},{9,8},{10,11... | collective-permute-start | bytes 12296 | tf_op jit(solution)/shard_map/ppermute | solution.py:398
  56.9 1.0 copy-start.3
  57.8 17.3 %copy-start = (bf16[1024,512]{1,0:T(8,128)(2,1)S(1)}, bf16[1024,512]{1,0:T(8,128)(2,1)}, u32[]{:S(2)}) copy-start(bf16[1024,512]{1,0:T(8,128)(2,1)} %get-tuple-element.7.kv0) | copy-start | bytes 3145732
  73.6 38.4 %collective-permute-start.6 = (bf16[512,1024]{1,0:T(8,128)(2,1)}, bf16[512,1024]{1,0:T(8,128)(2,1)}, u32[]{:S(2)}, u32[]{:S(2)}) collective-permute-start(bf16[512,1024]{1,0:T(8,128)(2,1)} %attend.2.oa_hbm), channel_id=1, source_target_pairs={{0,4},{4,8},{8,12},{12,0},{1,5},{5,9},{9,13},{13,1},{2,6},{6,10},{... | collective-permute-start | bytes 3145736 | tf_op jit(solution)/shard_map/ppermute | solution.py:449
Sparse Core Ops, SparseCore 0:
  9.7 92.3 all-gather.2

commit v2 on v1

--- a/solution.py
+++ b/solution.py
@@ -33,43 +33,124 @@
     return (x * cos_tab + pltpu.roll(x, HEAD // 2, 1) * sin_tab).astype(jnp.bfloat16)
 
 
-def kv_kernel(x_ref, gain_ref, wk_ref, wv_ref, cos_ref, sin_ref, normed_ref, kv_ref):
-    x = x_ref[...].astype(jnp.float32)
-    var = jnp.mean(x * x, axis=-1, keepdims=True)
-    normed = (x * lax.rsqrt(var + EPS) * gain_ref[...]).astype(jnp.bfloat16)
-    normed_ref[...] = normed
-    n_k = wk_ref.shape[1]
-    k = jnp.dot(normed, wk_ref[...], preferred_element_type=jnp.float32)
-    v = jnp.dot(normed, wv_ref[...], preferred_element_type=jnp.float32)
-    for h in range(n_k // HEAD):
-        cols = slice(h * HEAD, (h + 1) * HEAD)
-        kv_ref[:, cols] = rotate(k[:, cols], cos_ref[...], sin_ref[...])
-    kv_ref[:, n_k:] = v.astype(jnp.bfloat16)
-
-
-def q_kernel(normed_ref, wq_ref, cos_ref, sin_ref, q_ref):
-    for c in range(0, wq_ref.shape[1], 2 * HEAD):
-        q = jnp.dot(normed_ref[...], wq_ref[:, c:c + 2 * HEAD], preferred_element_type=jnp.float32)
-        for h in range(2):
-            q_ref[:, c + h * HEAD:c + (h + 1) * HEAD] = rotate(q[:, h * HEAD:(h + 1) * HEAD], cos_ref[...], sin_ref[...])
-
-
-def attn_kernel(first, kmin_ref, kmax_ref, qmin_ref, qmax_ref, q_ref, posq_ref, posk_ref, kv0, kv1, kv2, kv3, o_ref,
-                kv_s, q_s, pq_s, m_s, l_s, acc_s, full_l, part_l, sems):
+FRONT_ROWS = 256
+FRONT_COLS = 256
+
+
+def front_kernel(n_cp, x_hbm, pos_hbm, gain_ref, wk_hbm, wv_hbm, wq_hbm, cos_ref, sin_ref, kv_hbm, pos_out, q_hbm,
+                 x_t, normed, wkv, wq_v, kv_t, q_t, x_sem, w_sem, kv_sem, q_sem, p_send, p_recv, s_send, s_recv):
+    mesh_id = pl.DeviceIdType.MESH
+    cp = lax.axis_index("cp")
+    core, chip = cp % 2, cp // 2
+    cp_p, cp_y = cp + 1 - 2 * core, cp + 2 - 4 * chip
+    to_p, to_y, to_d = {"cp": cp_p}, {"cp": cp_y}, {"cp": cp_y + 1 - 2 * core}
+    rows = normed.shape[0]
+    k_cols = wk_hbm.shape[1]
+    n_rb = rows // FRONT_ROWS
+    n_cb = wq_hbm.shape[1] // FRONT_COLS
+
+    def x_load(r):
+        return pltpu.make_async_copy(x_hbm.at[pl.ds(r * FRONT_ROWS, FRONT_ROWS), :], x_t.at[r % 2], x_sem.at[r % 2])
+
+    weights = [pltpu.make_async_copy(wk_hbm, wkv.at[:, pl.ds(0, k_cols)], w_sem.at[0]),
+               pltpu.make_async_copy(wv_hbm, wkv.at[:, pl.ds(k_cols, k_cols)], w_sem.at[1]),
+               pltpu.make_async_copy(wq_hbm, wq_v, w_sem.at[2])]
+    x_load(0).start()
+    weights[0].start()
+    weights[1].start()
+    x_load(1).start()
+    weights[2].start()
+
+    barrier = pltpu.get_barrier_semaphore()
+    for peer in (to_p, to_y, to_d):
+        pl.semaphore_signal(barrier, inc=1, device_id=peer, device_id_type=mesh_id)
+    pl.semaphore_wait(barrier, 3)
+
+    pos_copies = [pltpu.make_async_remote_copy(src_ref=pos_hbm, dst_ref=pos_out.at[i], send_sem=p_send.at[i], recv_sem=p_recv.at[i],
+                                               device_id=peer, device_id_type=mesh_id) for i, peer in enumerate((to_p, to_y, to_d))]
+    for c in pos_copies:
+        c.start()
+
+    def send(kind, r):
+        src = (0, 0, 2)[kind] * rows + r * FRONT_ROWS
+        dst = (1, 2, 3)[kind] * rows + r * FRONT_ROWS
+        return pltpu.make_async_remote_copy(src_ref=kv_hbm.at[pl.ds(src, FRONT_ROWS), :], dst_ref=kv_hbm.at[pl.ds(dst, FRONT_ROWS), :],
+                                            send_sem=s_send.at[kind, r], recv_sem=s_recv.at[kind, r],
+                                            device_id=(to_p, to_y, to_p)[kind], device_id_type=mesh_id)
+
+    def kv_store(r):
+        return pltpu.make_async_copy(kv_t.at[r], kv_hbm.at[pl.ds(r * FRONT_ROWS, FRONT_ROWS), :], kv_sem.at[r])
+
+    def spread(r):
+        kv_store(r).wait()
+        send(1, r).start()
+        send(0, r).start()
+
+    for r in range(n_rb):
+        at = slice(r * FRONT_ROWS, (r + 1) * FRONT_ROWS)
+        x_load(r).wait()
+        x = x_t[r % 2].astype(jnp.float32)
+        var = jnp.mean(x * x, axis=-1, keepdims=True)
+        normed[at, :] = (x * lax.rsqrt(var + EPS) * gain_ref[...]).astype(jnp.bfloat16)
+        if r + 2 < n_rb:
+            x_load(r + 2).start()
+        if r == 0:
+            weights[0].wait()
+            weights[1].wait()
+        kv = jnp.dot(normed[at, :], wkv[...], preferred_element_type=jnp.float32)
+        for h in range(k_cols // HEAD):
+            kv_t[r, :, h * HEAD:(h + 1) * HEAD] = rotate(kv[:, h * HEAD:(h + 1) * HEAD], cos_ref[at, :], sin_ref[at, :])
+        kv_t[r, :, k_cols:] = kv[:, k_cols:].astype(jnp.bfloat16)
+        kv_store(r).start()
+        if r > 0:
+            spread(r - 1)
+
+    weights[2].wait()
+
+    def q_store(c):
+        return pltpu.make_async_copy(q_t.at[c % 2], q_hbm.at[:, pl.ds(c * FRONT_COLS, FRONT_COLS)], q_sem.at[c % 2])
+
+    for c in range(n_cb):
+        if c == 0:
+            spread(n_rb - 1)
+        if c >= 2:
+            q_store(c - 2).wait()
+        q = jnp.dot(normed[...], wq_v[:, c * FRONT_COLS:(c + 1) * FRONT_COLS], preferred_element_type=jnp.float32)
+        for h in range(FRONT_COLS // HEAD):
+            q_t[c % 2, :, h * HEAD:(h + 1) * HEAD] = rotate(q[:, h * HEAD:(h + 1) * HEAD], cos_ref[...], sin_ref[...])
+        q_store(c).start()
+        if c < n_rb:
+            send(1, c).wait_recv()
+            send(2, c).start()
+    for r in range(n_cb, n_rb):
+        send(1, r).wait_recv()
+        send(2, r).start()
+
+    q_store(n_cb - 2).wait()
+    q_store(n_cb - 1).wait()
+    for r in range(n_rb):
+        send(0, r).wait_recv()
+        send(2, r).wait_recv()
+    for c in pos_copies:
+        c.wait()
+    for kind in range(3):
+        for r in range(n_rb):
+            send(kind, r).wait_send()
+
+
+def attn_kernel(first, kmin_ref, kmax_ref, qmin_ref, qmax_ref, q_ref, posq_ref, posk_ref, kv_hbm, o_ref,
+                kv_s, q_s, pq_s, m_s, l_s, acc_s, full_l, part_l, sem):
     step = pl.program_id(0)
-    rows = kv0.shape[0]
     n_blocks = kmin_ref.shape[0]
-    n_kv = kv0.shape[1] // (2 * HEAD)
+    n_kv = kv_hbm.shape[1] // (2 * HEAD)
     n_heads = q_ref.shape[1] // HEAD
     per_kv = n_heads // n_kv
 
     @pl.when(step == 0)
     def _():
-        copies = [pltpu.make_async_copy(src, kv_s.at[pl.ds(i * rows, rows), :], sems.at[i]) for i, src in enumerate((kv0, kv1, kv2, kv3))]
-        for c in copies:
-            c.start()
-        for c in copies:
-            c.wait()
+        load = pltpu.make_async_copy(kv_hbm, kv_s, sem)
+        load.start()
+        load.wait()
 
     q_lo = qmin_ref[first + step]
     q_hi = qmax_ref[first + step]
@@ -364,8 +445,6 @@
     n_tp, n_cp, n_dp = mesh.shape["tp"], mesh.shape["cp"], mesh.shape["dp"]
     plane = n_dp * n_cp
     ring = [(i, (i + 1) % n_tp) for i in range(n_tp)]
-    swap_core = [(i, i ^ 1) for i in range(n_cp)]
-    swap_chip = [(i, i ^ 2) for i in range(n_cp)]
 
     def local_block(hidden, tok_pos, norm_gain, w_query, w_key, w_value, w_out):
         rows, width = hidden.shape
@@ -378,45 +457,44 @@
         z_slices = lax.all_gather(own_slice, "tp", axis=0, tiled=False)
 
         cos_tab, sin_tab = rope_tables(tok_pos)
-        rb = 256
-        row_blk = lambda cols: pl.BlockSpec((rb, cols), lambda i: (i, 0))
-        whole = lambda r, c: pl.BlockSpec((r, c), lambda i: (0, 0))
-        normed, kv = pl.pallas_call(
-            kv_kernel,
-            grid=(rows // rb,),
-            out_shape=(jax.ShapeDtypeStruct((rows, width), jnp.bfloat16), jax.ShapeDtypeStruct((rows, 2 * k_cols), jnp.bfloat16)),
-            in_specs=[row_blk(width), whole(1, width), whole(width, k_cols), whole(width, k_cols), row_blk(HEAD), row_blk(HEAD)],
-            out_specs=(row_blk(width), row_blk(2 * k_cols)),
-            cost_estimate=pl.CostEstimate(flops=4 * rows * width * k_cols, bytes_accessed=24 << 20, transcendentals=0),
-            name="norm_kv",
-        )(hidden, norm_gain.reshape(1, width), w_key, w_value, cos_tab, sin_tab)
-
+        smem = pl.BlockSpec(memory_space=pltpu.SMEM)
+        anym = pl.BlockSpec(memory_space=pl.ANY)
+        vmem = pl.BlockSpec(memory_space=pltpu.VMEM)
         pos_row = tok_pos.reshape(rows // KB, 1, KB)
-        kv_core = lax.ppermute(kv, "cp", swap_core)
-        kv_chip = lax.ppermute(kv, "cp", swap_chip)
-        swap_diag = [(i, i ^ 3) for i in range(n_cp)]
-        pos_rel = jnp.concatenate([pos_row] + [lax.ppermute(pos_row, "cp", pairs) for pairs in (swap_core, swap_chip, swap_diag)], axis=0)
-
-        q_rot = pl.pallas_call(
-            q_kernel,
-            grid=(rows // rb,),
-            out_shape=jax.ShapeDtypeStruct((rows, q_cols), jnp.bfloat16),
-            in_specs=[row_blk(width), whole(width, q_cols), row_blk(HEAD), row_blk(HEAD)],
-            out_specs=row_blk(q_cols),
-            cost_estimate=pl.CostEstimate(flops=2 * rows * width * q_cols, bytes_accessed=20 << 20, transcendentals=0),
-            name="q_rope",
-        )(normed, w_query, cos_tab, sin_tab)
-
-        kv_chip, q_rot = lax.optimization_barrier((kv_chip, q_rot))
-        kv_diag = lax.ppermute(kv_chip, "cp", swap_core)
+        n_rb = rows // FRONT_ROWS
+        kv_all, pos_far, q_rot = pl.pallas_call(
+            functools.partial(front_kernel, n_cp),
+            out_shape=(jax.ShapeDtypeStruct((n_cp * rows, 2 * k_cols), jnp.bfloat16), jax.ShapeDtypeStruct((n_cp - 1,) + pos_row.shape, jnp.int32),
+                       jax.ShapeDtypeStruct((rows, q_cols), jnp.bfloat16)),
+            in_specs=[anym, anym, vmem, anym, anym, anym, vmem, vmem],
+            out_specs=(anym, anym, anym),
+            scratch_shapes=[
+                pltpu.VMEM((2, FRONT_ROWS, width), jnp.bfloat16),
+                pltpu.VMEM((rows, width), jnp.bfloat16),
+                pltpu.VMEM((width, 2 * k_cols), jnp.bfloat16),
+                pltpu.VMEM((width, q_cols), jnp.bfloat16),
+                pltpu.VMEM((n_rb, FRONT_ROWS, 2 * k_cols), jnp.bfloat16),
+                pltpu.VMEM((2, rows, FRONT_COLS), jnp.bfloat16),
+                pltpu.SemaphoreType.DMA((2,)),
+                pltpu.SemaphoreType.DMA((3,)),
+                pltpu.SemaphoreType.DMA((n_rb,)),
+                pltpu.SemaphoreType.DMA((2,)),
+                pltpu.SemaphoreType.DMA((n_cp - 1,)),
+                pltpu.SemaphoreType.DMA((n_cp - 1,)),
+                pltpu.SemaphoreType.DMA((3, n_rb)),
+                pltpu.SemaphoreType.DMA((3, n_rb)),
+            ],
+            compiler_params=pltpu.CompilerParams(collective_id=1, has_side_effects=True, vmem_limit_bytes=63 << 20),
+            cost_estimate=pl.CostEstimate(flops=2 * rows * width * (q_cols + 2 * k_cols), bytes_accessed=24 << 20, transcendentals=0),
+            name="front",
+        )(hidden, pos_row, norm_gain.reshape(1, width), w_key, w_value, w_query, cos_tab, sin_tab)
+        pos_rel = jnp.concatenate([pos_row, pos_far.reshape(-1, 1, KB)], axis=0)
 
         kmin, kmax = jnp.min(pos_rel, axis=(1, 2)), jnp.max(pos_rel, axis=(1, 2))
         n_q = rows // QB
         qpos = tok_pos.reshape(n_q, QB)
         qmin, qmax = jnp.min(qpos, axis=1), jnp.max(qpos, axis=1)
         pos_col = tok_pos.reshape(rows, 1)
-        smem = pl.BlockSpec(memory_space=pltpu.SMEM)
-        anym = pl.BlockSpec(memory_space=pl.ANY)
 
         def attend(part, n_parts):
             steps = n_q // n_parts
@@ -428,7 +506,7 @@
                 grid=(steps,),
                 out_shape=jax.ShapeDtypeStruct((rows // n_parts, q_cols), jnp.bfloat16),
                 in_specs=[smem] * 4 + [pl.BlockSpec((QB, q_cols), lambda i: (first + i, 0)), pl.BlockSpec((QB, 1), lambda i: (first + i, 0)),
-                                       pl.BlockSpec(pos_rel.shape, lambda i: (0, 0, 0))] + [anym] * 4,
+                                       pl.BlockSpec(pos_rel.shape, lambda i: (0, 0, 0)), anym],
                 out_specs=pl.BlockSpec((QB, q_cols), lambda i: (i, 0)),
                 scratch_shapes=[
                     pltpu.VMEM((n_cp * rows, 2 * k_cols), jnp.bfloat16),
@@ -439,11 +517,11 @@
                     pltpu.VMEM((n_rows, HEAD), jnp.float32),
                     pltpu.SMEM((blocks_max + WIDE,), jnp.int32),
                     pltpu.SMEM((blocks_max + WIDE + GROUP,), jnp.int32),
-                    pltpu.SemaphoreType.DMA((4,)),
+                    pltpu.SemaphoreType.DMA,
                 ],
                 cost_estimate=pl.CostEstimate(flops=4 * rows // n_parts * n_cp * rows * q_cols, bytes_accessed=8 << 20, transcendentals=0),
                 name="attend",
-            )(kmin, kmax, qmin, qmax, q_rot, pos_col, pos_rel, kv, kv_core, kv_chip, kv_diag)
+            )(kmin, kmax, qmin, qmax, q_rot, pos_col, pos_rel, kv_all)
 
         o_a = attend(0, 2)
         left_a = lax.ppermute(o_a, "tp", ring)
@@ -473,8 +551,8 @@
             cost_estimate=pl.CostEstimate(flops=2 * n_tp * rows * q_cols * width, bytes_accessed=48 << 20, transcendentals=0),
             name="out_gather",
         )(o_a, o_b, left_a, w_out, z_slices, hidden)
-        k_cache = kv[:, :k_cols].reshape(rows, n_kv, HEAD)
-        v_cache = kv[:, k_cols:].reshape(rows, n_kv, HEAD)
+        k_cache = kv_all[:rows, :k_cols].reshape(rows, n_kv, HEAD)
+        v_cache = kv_all[:rows, k_cols:].reshape(rows, n_kv, HEAD)
         return hidden_out, k_cache, v_cache
 
     row_spec = P(("dp", "cp"), None)

time: 262 us -> 261 us (level)
  Pallas kernels: 197 us -> 219 us
  waiting for transfers between devices: 22.2 us -> 4.71 us
  starting transfers between devices: 7.87 us -> 1.39 us
    pallas_call x2, Pallas kernels: 36.1 us -> 51.5 us  [attend(): pl.pallas_call(functools.partial(attn_kernel, first), grid=(steps,), out_...]
    ppermute x1, waiting for transfers between devices: 14.6 us -> 4.69 us  [local_block(): left_a = lax.ppermute(o_a, 'tp', ring)]
    pallas_call x2 -> x1, Pallas kernels: 26.1 us -> 35.1 us  [local_block(): pl.pallas_call(functools.partial(front_kernel, n_cp), out_shape=(jax.Shap...]
    ppermute x6 -> x0, waiting for transfers between devices: 7.59 us -> none  [the longest x1 7.17 us: local_block(): kv_chip = lax.ppermute(kv, 'cp', swap_chip)]
    ppermute x6 -> x0, starting transfers between devices: 6.31 us -> none  [the longest x3 2.14 us: local_block(): lax.ppermute(pos_row, 'cp', pairs)]
    unnamed x9 -> x3, local copies, waits for them, and re-layouts: 8.87 us -> 7.89 us
  transfers between devices with their start and end apart: 8 -> 2, of which waited for: 3 -> 1; matrix products, arithmetic and copies ran while one was open for 4% -> 5% of each run, Pallas kernels for 24% -> 33%
where the time goes in v2:
time: 261 us; the launch traced here: 262 us
  Pallas kernels  219 us (84%)
  local copies, waits for them, and re-layouts  15 us (6%)
  between operations  14.1 us (5%)
  other arithmetic  7.76 us (3%)
  waiting for transfers between devices  4.71 us (2%)
    pallas_call x1, Pallas kernels, local_block(): pl.pallas_call(functools.partial(out_kernel, n_tp, n_cp), out_shape=jax.S...  132 us
    pallas_call x2, Pallas kernels, attend(): pl.pallas_call(functools.partial(attn_kernel, first), grid=(steps,), out_...  51.5 us
    pallas_call x1, Pallas kernels, local_block(): pl.pallas_call(functools.partial(front_kernel, n_cp), out_shape=(jax.Shap...  35.1 us
    unnamed x3, local copies, waits for them, and re-layouts  7.89 us
  transfers between devices with their start and end apart: 2, of which 1 were waited for; matrix products, arithmetic and copies ran while one was open for 5% of the time, Pallas kernels for 33%

profile of v2, /device:TPU:1, one launch (start us, length us, event | category | flops | bytes accessed | tf_op | source)
XLA Modules:
  0.0 261.7 jit_solution(13549556970184778613)
XLA Ops:
  7.2 0.0 all-gather.3.cloned.1.call-start
  7.2 2.3 constant_dynamic-slice_fusion
  9.5 0.0 all-gather.3.cloned.1.call-update
  9.6 0.7 convert_element_type.3
  10.3 1.7 copy.12.posq_ref
  12.0 0.1 compare_select_fusion
  12.0 1.4 bitcast_reduce_fusion
  13.5 3.0 %fusion = (f32[1024,128]{1,0:T(8,128)}, f32[1024,128]{1,0:T(8,128)}) fusion(f32[128]{0:T(128)S(1)} %get-tuple-element.18, f32[128]{0:T(128)S(1)} %get-tuple-element.19, f32[1024]{0:T(1024)S(1)} %convert_element_type.3), kind=kLoop, calls=%fused_computation.2 | loop fusion | flops 262144 | bytes 1053696 | tf_op jit(solution)/shard_map/mul | solution.py:28
  16.5 0.0 copy-start
  16.5 35.1 %front.1 = (bf16[4096,512]{1,0:T(8,128)(2,1)}, s32[3,8,1,128]{3,2,1,0:T(1,128)}, bf16[1024,1024]{1,0:T(8,128)(2,1)}) custom-call(bf16[1024,4096]{1,0:T(8,128)(2,1)} %x_hbm.3, s32[8,1,128]{2,1,0:T(1,128)} %bitcast.9, f32[1,4096]{1,0:T(1,128)} %bitcast.13, bf16[4096,256]{1,0:T(8,128)(2,1)} %wk_hbm.1, bf16[4096,256]{1,0:T(8,128)(2,1)} %wv_hbm.1, ...), custom_call_target="tpu_custom_call" | custom-call | flops 12884901888 | bytes 25165824 | tf_op jit(solution)/shard_map/front/pallas_call | solution.py:465
  51.6 0.0 copy-done
  51.6 2.5 fusion.1
  54.1 24.0 %attend.2.oa_hbm = bf16[512,1024]{1,0:T(8,128)(2,1)} custom-call(s32[32]{0:T(128)} %get-tuple-element.10.kmin_ref, s32[32]{0:T(128)} %get-tuple-element.9.kmax_ref, s32[8]{0:T(128)} %get-tuple-element.12.qmin_ref, s32[8]{0:T(128)} %get-tuple-element.11.qmax_ref, bf16[1024,1024]{1,0:T(8,128)(2,1)} %get-tuple-element.7.q_ref, s32[1024,1]{1,0:T(8,128)} %copy.12.posq_ref, ...), custom_call_target="tpu_custom_call" | custom-call | flops 8589934592 | bytes 8388608 | tf_op jit(solution)/shard_map/attend/pallas_call | solution.py:504
  78.1 1.4 collective-permute-start
  79.4 1.3 fusion.2
  80.7 0.9 reshape.40
  81.6 0.9 reshape.39
  82.5 27.5 %attend.3.ob_hbm = bf16[512,1024]{1,0:T(8,128)(2,1)} custom-call(s32[32]{0:T(128)} %get-tuple-element.10.kmin_ref, s32[32]{0:T(128)} %get-tuple-element.9.kmax_ref, s32[8]{0:T(128)} %get-tuple-element.12.qmin_ref, s32[8]{0:T(128)} %get-tuple-element.11.qmax_ref, bf16[1024,1024]{1,0:T(8,128)(2,1)} %get-tuple-element.7.q_ref, s32[1024,1]{1,0:T(8,128)} %copy.12.posq_ref, ...), custom_call_target="tpu_custom_call" | custom-call | flops 8589934592 | bytes 8388608 | tf_op jit(solution)/shard_map/attend/pallas_call | solution.py:504
  110.1 4.7 %collective-permute-done.la_hbm = bf16[512,1024]{1,0:T(8,128)(2,1)} collective-permute-done((bf16[512,1024]{1,0:T(8,128)(2,1)}, bf16[512,1024]{1,0:T(8,128)(2,1)}, u32[]{:S(2)}, u32[]{:S(2)}) %collective-permute-start) | collective-permute-done | bytes 1048608 | tf_op jit(solution)/shard_map/ppermute | solution.py:527
  114.7 0.0 all-gather.3.cloned.1.call-done
  114.8 132.2 %out_gather.1 = bf16[1024,4096]{1,0:T(8,128)(2,1)} custom-call(bf16[512,1024]{1,0:T(8,128)(2,1)} %attend.2.oa_hbm, bf16[512,1024]{1,0:T(8,128)(2,1)} %attend.3.ob_hbm, bf16[512,1024]{1,0:T(8,128)(2,1)} %collective-permute-done.la_hbm, bf16[1024,4096]{1,0:T(8,128)(2,1)} %w_hbm.1, bf16[4,128,4096]{2,1,0:T(8,128)(2,1)} %bitcast.12, bf16[1024,4096]{1,0:T(8,128)(2,1)} %x_hbm.3), custom_call_target="tpu_custom_call" | custom-call | flops 34359738368 | bytes 50331648 | tf_op jit(solution)/shard_map/out_gather/pallas_call | solution.py:529
  247.0 7.9 %copy.15 = bf16[1024,4096]{1,0:T(8,128)(2,1)} copy(bf16[1024,4096]{1,0:T(8,128)(2,1)} %out_gather.1) | data formatting | bytes 16777216
  (1 shorter events, 0.0 us)
Async XLA Ops:
  7.2 107.6 %all-gather.3.cloned.1.call-start = ((), (), s32[]{:S(2)}) async-start(), calls=%async_computation | async-start | bytes 5242880 | tf_op jit(solution)/shard_map/all_gather | solution.py:457
  16.5 35.1 %copy-start = (s32[1024]{0:T(1024)S(1)}, s32[1024]{0:T(1024)}, u32[]{:S(2)}) copy-start(s32[1024]{0:T(1024)} %param.8) | copy-start | bytes 12292
  78.1 36.7 %collective-permute-start = (bf16[512,1024]{1,0:T(8,128)(2,1)}, bf16[512,1024]{1,0:T(8,128)(2,1)}, u32[]{:S(2)}, u32[]{:S(2)}) collective-permute-start(bf16[512,1024]{1,0:T(8,128)(2,1)} %attend.2.oa_hbm), channel_id=1, source_target_pairs={{0,4},{4,8},{8,12},{12,0},{1,5},{5,9},{9,13},{13,1},{2,6},{6,10},{... | collective-permute-start | bytes 3145736 | tf_op jit(solution)/shard_map/ppermute | solution.py:527
Sparse Core Ops, SparseCore 0:
  9.7 92.5 all-gather.2

commit v3 on v2

--- a/solution.py
+++ b/solution.py
@@ -7,6 +7,7 @@
 from jax.experimental import pallas as pl
 from jax.experimental.pallas import tpu as pltpu
 from jax.sharding import PartitionSpec as P
+
 
 HEAD = 128
 THETA = 1000000
@@ -37,10 +38,11 @@
 FRONT_COLS = 256
 
 
-def front_kernel(n_cp, x_hbm, pos_hbm, gain_ref, wk_hbm, wv_hbm, wq_hbm, cos_ref, sin_ref, kv_hbm, pos_out, q_hbm,
-                 x_t, normed, wkv, wq_v, kv_t, q_t, x_sem, w_sem, kv_sem, q_sem, p_send, p_recv, s_send, s_recv):
+def front_kernel(n_tp, n_cp, slice_rows, x_hbm, pos_hbm, gain_ref, wk_hbm, wv_hbm, wq_hbm, wo_hbm, cos_ref, sin_ref, kv_hbm, pos_out, q_hbm, wz_hbm, relay_hbm,
+                 x_t, normed, wkv, wq_v, kv_t, q_t, x_sem, w_sem, kv_sem, q_sem, p_send, p_recv, s_send, s_recv, z_send, z_recv):
     mesh_id = pl.DeviceIdType.MESH
-    cp = lax.axis_index("cp")
+    tp, dp, cp = lax.axis_index("tp"), lax.axis_index("dp"), lax.axis_index("cp")
+    to_right, to_left = {"tp": (tp + 1) % n_tp}, {"tp": (tp + n_tp - 1) % n_tp}
     core, chip = cp % 2, cp // 2
     cp_p, cp_y = cp + 1 - 2 * core, cp + 2 - 4 * chip
     to_p, to_y, to_d = {"cp": cp_p}, {"cp": cp_y}, {"cp": cp_y + 1 - 2 * core}
@@ -62,9 +64,22 @@
     weights[2].start()
 
     barrier = pltpu.get_barrier_semaphore()
-    for peer in (to_p, to_y, to_d):
+    for peer in (to_p, to_y, to_d, to_right, to_left):
         pl.semaphore_signal(barrier, inc=1, device_id=peer, device_id_type=mesh_id)
-    pl.semaphore_wait(barrier, 3)
+    pl.semaphore_wait(barrier, 5)
+
+    hs = slice_rows // 2
+    own = (dp * n_cp + cp) * slice_rows
+
+    def z_copy(i):
+        src, dst = ((wo_hbm.at[pl.ds(pl.multiple_of(own, hs), hs), :], wz_hbm),
+                    (wo_hbm.at[pl.ds(pl.multiple_of(own + hs, hs), hs), :], relay_hbm.at[0]),
+                    (wz_hbm, relay_hbm.at[1]))[i]
+        return pltpu.make_async_remote_copy(src_ref=src, dst_ref=dst, send_sem=z_send.at[i], recv_sem=z_recv.at[i],
+                                            device_id=to_right, device_id_type=mesh_id)
+
+    z_copy(0).start()
+    z_copy(1).start()
 
     pos_copies = [pltpu.make_async_remote_copy(src_ref=pos_hbm, dst_ref=pos_out.at[i], send_sem=p_send.at[i], recv_sem=p_recv.at[i],
                                                device_id=peer, device_id_type=mesh_id) for i, peer in enumerate((to_p, to_y, to_d))]
@@ -106,6 +121,8 @@
             spread(r - 1)
 
     weights[2].wait()
+    z_copy(0).wait_recv()
+    z_copy(2).start()
 
     def q_store(c):
         return pltpu.make_async_copy(q_t.at[c % 2], q_hbm.at[:, pl.ds(c * FRONT_COLS, FRONT_COLS)], q_sem.at[c % 2])
@@ -133,6 +150,10 @@
         send(2, r).wait_recv()
     for c in pos_copies:
         c.wait()
+    z_copy(1).wait_recv()
+    z_copy(2).wait_recv()
+    for i in range(3):
+        z_copy(i).wait_send()
     for kind in range(3):
         for r in range(n_rb):
             send(kind, r).wait_send()
@@ -255,8 +276,8 @@
 N_CHUNK = 4
 
 
-def out_kernel(n_tp, n_cp, oa_hbm, ob_hbm, la_hbm, w_hbm, z_hbm, x_hbm, out_hbm, o_buf, w_buf, acc, w_t, x_t, y_t,
-               o_send, o_recv, w_send, w_recv, w_local, ld_sem, st_sem, own_sem):
+def out_kernel(n_tp, n_cp, sl, oa_hbm, ob_hbm, la_hbm, w_hbm, wz_hbm, relay_hbm, relay2_hbm, x_hbm, out_hbm, o_buf, w_buf, acc, w_t, x_t, y_t,
+               o_send, o_recv, w_send, w_recv, w_local, ld_sem, st_sem, own_sem, z_send, z_recv):
     mesh_id = pl.DeviceIdType.MESH
     tp, dp, cp = lax.axis_index("tp"), lax.axis_index("dp"), lax.axis_index("cp")
     core, chip = cp % 2, cp // 2
@@ -264,7 +285,6 @@
     to_right, to_left = {"tp": (tp + 1) % n_tp}, {"tp": (tp + n_tp - 1) % n_tp}
     to_x, to_y, to_p = {"dp": 1 - dp}, {"cp": cp_y}, {"cp": cp + 1 - 2 * core}
     p_me, p_x, p_y, p_d = dp * n_cp + cp, (1 - dp) * n_cp + cp, dp * n_cp + cp_y, (1 - dp) * n_cp + cp_y
-    sl = z_hbm.shape[1]
     n_rows, width = acc.shape
     half = n_rows // 2
     ch = n_rows // N_CHUNK
@@ -292,24 +312,34 @@
 
     def w_copy(k, kind):
         hs = sl // 2
-        own = z_hbm.at[(tp + n_tp - k - 1) % n_tp]
         idx, peer, where = {
             "own_x": (0, to_x, rows(p_me)), "own_y": (1, to_y, rows(p_me)), "own_p": (2, to_p, rows(p_me)),
             "dx": (3, to_x, rows(p_y, hs, hs)), "dy": (4, to_y, rows(p_x, 0, hs)),
             "px": (5, to_p, rows(p_x)), "py": (6, to_p, rows(p_y)),
             "pd0": (7, to_p, rows(p_d, 0, hs)), "pd1": (8, to_p, rows(p_d, hs, hs)),
         }[kind]
-        src = own if idx < 3 else w_buf.at[k, where, :]
-        return pltpu.make_async_remote_copy(src_ref=src, dst_ref=w_buf.at[k, where, :], send_sem=w_send.at[k, idx],
+        at = w_buf.at[k, where, :]
+        return pltpu.make_async_remote_copy(src_ref=at, dst_ref=at, send_sem=w_send.at[k, idx],
                                             recv_sem=w_recv.at[k, idx], device_id=peer, device_id_type=mesh_id)
 
-    def w_own_local(k):
-        return pltpu.make_async_copy(z_hbm.at[(tp + n_tp - k - 1) % n_tp], w_buf.at[k, rows(p_me), :], w_local.at[k])
+    hs = sl // 2
+
+    def w_own_half(k, h):
+        src = ((wz_hbm, relay_hbm.at[0]), (relay_hbm.at[1], relay2_hbm.at[0]), (relay2_hbm.at[1], None))[k][h]
+        return pltpu.make_async_copy(src, w_buf.at[k, rows(p_me, h * hs, hs), :], w_local.at[k, h])
+
+    def w_last_half():
+        return pltpu.make_async_remote_copy(src_ref=relay2_hbm.at[0], dst_ref=w_buf.at[last - 1, rows(p_me, hs, hs), :], send_sem=z_send,
+                                            recv_sem=z_recv, device_id=to_right, device_id_type=mesh_id)
 
     def start_own(k):
+        w_own_half(k, 0).wait()
+        if k < last - 1:
+            w_own_half(k, 1).wait()
+        else:
+            w_last_half().wait_recv()
         for kind in ("own_x", "own_y", "own_p"):
             w_copy(k, kind).start()
-        w_own_local(k).start()
 
     def pass_on(k):
         w_copy(k, "own_x").wait_recv()
@@ -324,7 +354,6 @@
         w_copy(k, "pd1").start()
 
     def complete(k):
-        w_own_local(k).wait()
         for kind in ("own_p", "px", "py", "pd0", "pd1"):
             w_copy(k, kind).wait_recv()
 
@@ -344,8 +373,13 @@
 
         lax.fori_loop(0, n_tile, body, 0)
 
+    for k in range(last):
+        w_own_half(k, 0).start()
+        if k < last - 1:
+            w_own_half(k, 1).start()
     for c in (0, 1):
         o_copy(1, c).start()
+    w_last_half().start()
     for c in (2, 3):
         o_copy(0, c).start()
     start_own(0)
@@ -439,6 +473,7 @@
                 o_copy(s, c).wait_send()
         for kind in ("own_x", "own_y", "own_p", "dx", "dy", "px", "py", "pd0", "pd1"):
             w_copy(s, kind).wait_send()
+    w_last_half().wait_send()
 
 
 def solution(mesh):
@@ -450,24 +485,20 @@
         rows, width = hidden.shape
         q_cols, k_cols = w_query.shape[1], w_key.shape[1]
         n_kv = k_cols // HEAD
-        plane_idx = lax.axis_index("dp") * n_cp + lax.axis_index("cp")
-
         slice_rows = w_out.shape[0] // plane
-        own_slice = lax.dynamic_slice_in_dim(w_out, plane_idx * slice_rows, slice_rows, axis=0)
-        z_slices = lax.all_gather(own_slice, "tp", axis=0, tiled=False)
-
         cos_tab, sin_tab = rope_tables(tok_pos)
         smem = pl.BlockSpec(memory_space=pltpu.SMEM)
         anym = pl.BlockSpec(memory_space=pl.ANY)
         vmem = pl.BlockSpec(memory_space=pltpu.VMEM)
         pos_row = tok_pos.reshape(rows // KB, 1, KB)
         n_rb = rows // FRONT_ROWS
-        kv_all, pos_far, q_rot = pl.pallas_call(
-            functools.partial(front_kernel, n_cp),
+        kv_all, pos_far, q_rot, wz, relay = pl.pallas_call(
+            functools.partial(front_kernel, n_tp, n_cp, slice_rows),
             out_shape=(jax.ShapeDtypeStruct((n_cp * rows, 2 * k_cols), jnp.bfloat16), jax.ShapeDtypeStruct((n_cp - 1,) + pos_row.shape, jnp.int32),
-                       jax.ShapeDtypeStruct((rows, q_cols), jnp.bfloat16)),
-            in_specs=[anym, anym, vmem, anym, anym, anym, vmem, vmem],
-            out_specs=(anym, anym, anym),
+                       jax.ShapeDtypeStruct((rows, q_cols), jnp.bfloat16), jax.ShapeDtypeStruct((slice_rows // 2, width), jnp.bfloat16),
+                       jax.ShapeDtypeStruct((2, slice_rows // 2, width), jnp.bfloat16)),
+            in_specs=[anym, anym, vmem, anym, anym, anym, anym, vmem, vmem],
+            out_specs=(anym,) * 5,
             scratch_shapes=[
                 pltpu.VMEM((2, FRONT_ROWS, width), jnp.bfloat16),
                 pltpu.VMEM((rows, width), jnp.bfloat16),
@@ -483,11 +514,14 @@
                 pltpu.SemaphoreType.DMA((n_cp - 1,)),
                 pltpu.SemaphoreType.DMA((3, n_rb)),
                 pltpu.SemaphoreType.DMA((3, n_rb)),
+                pltpu.SemaphoreType.DMA((3,)),
+                pltpu.SemaphoreType.DMA((3,)),
             ],
             compiler_params=pltpu.CompilerParams(collective_id=1, has_side_effects=True, vmem_limit_bytes=63 << 20),
             cost_estimate=pl.CostEstimate(flops=2 * rows * width * (q_cols + 2 * k_cols), bytes_accessed=24 << 20, transcendentals=0),
             name="front",
-        )(hidden, pos_row, norm_gain.reshape(1, width), w_key, w_value, w_query, cos_tab, sin_tab)
+        )(hidden, pos_row, norm_gain.reshape(1, width), w_key, w_value, w_query, w_out, cos_tab, sin_tab)
+        relay2 = lax.ppermute(relay, "tp", ring)
         pos_rel = jnp.concatenate([pos_row, pos_far.reshape(-1, 1, KB)], axis=0)
 
         kmin, kmax = jnp.min(pos_rel, axis=(1, 2)), jnp.max(pos_rel, axis=(1, 2))
@@ -527,9 +561,9 @@
         left_a = lax.ppermute(o_a, "tp", ring)
         o_b = attend(1, 2)
         hidden_out = pl.pallas_call(
-            functools.partial(out_kernel, n_tp, n_cp),
+            functools.partial(out_kernel, n_tp, n_cp, slice_rows),
             out_shape=jax.ShapeDtypeStruct((rows, width), jnp.bfloat16),
-            in_specs=[anym] * 6,
+            in_specs=[anym] * 8,
             out_specs=anym,
             scratch_shapes=[
                 pltpu.VMEM((n_tp, rows, q_cols), jnp.bfloat16),
@@ -542,15 +576,17 @@
                 pltpu.SemaphoreType.DMA((n_tp - 1, N_CHUNK)),
                 pltpu.SemaphoreType.DMA((n_tp - 1, 9)),
                 pltpu.SemaphoreType.DMA((n_tp - 1, 9)),
-                pltpu.SemaphoreType.DMA((n_tp - 1,)),
+                pltpu.SemaphoreType.DMA((n_tp - 1, 2)),
                 pltpu.SemaphoreType.DMA((2, 2)),
                 pltpu.SemaphoreType.DMA((2,)),
                 pltpu.SemaphoreType.DMA((3,)),
+                pltpu.SemaphoreType.DMA,
+                pltpu.SemaphoreType.DMA,
             ],
             compiler_params=pltpu.CompilerParams(collective_id=0, has_side_effects=True, vmem_limit_bytes=63 << 20),
             cost_estimate=pl.CostEstimate(flops=2 * n_tp * rows * q_cols * width, bytes_accessed=48 << 20, transcendentals=0),
             name="out_gather",
-        )(o_a, o_b, left_a, w_out, z_slices, hidden)
+        )(o_a, o_b, left_a, w_out, wz, relay, relay2, hidden)
         k_cache = kv_all[:rows, :k_cols].reshape(rows, n_kv, HEAD)
         v_cache = kv_all[:rows, k_cols:].reshape(rows, n_kv, HEAD)
         return hidden_out, k_cache, v_cache

time: 261 us -> 271 us (1.038)
  Pallas kernels: 219 us -> 235 us
  between operations: 14.1 us -> 0.72 us
  waiting for transfers between devices: 4.71 us -> 14.3 us
    pallas_call x2, Pallas kernels: 167 us -> 184 us  [the longest x1 142 us: local_block(): pl.pallas_call(functools.partial(out_kernel, n_tp, n_cp, slice_rows), out...]
    ppermute x0 -> x1, waiting for transfers between devices: none -> 14.3 us  [local_block(): relay2 = lax.ppermute(relay, 'tp', ring)]
    ppermute x1, waiting for transfers between devices: 4.69 us -> 0.01 us  [local_block(): left_a = lax.ppermute(o_a, 'tp', ring)]
    unnamed x3 -> x7, local copies, waits for them, and re-layouts: 7.89 us -> 7.9 us
  transfers between devices with their start and end apart: 2 -> 2, of which waited for: 1 -> 1; matrix products, arithmetic and copies ran while one was open for 5% -> 1% of each run, Pallas kernels for 33% -> 10%
where the time goes in v3:
time: 271 us
  Pallas kernels  235 us (87%)
  waiting for transfers between devices  14.3 us (5%)
  local copies, waits for them, and re-layouts  12.7 us (5%)
  other arithmetic  7.69 us (3%)
    pallas_call x1, Pallas kernels, local_block(): pl.pallas_call(functools.partial(out_kernel, n_tp, n_cp, slice_rows), out...  142 us
    pallas_call x2, Pallas kernels, attend(): pl.pallas_call(functools.partial(attn_kernel, first), grid=(steps,), out_...  51 us
    pallas_call x1, Pallas kernels, local_block(): pl.pallas_call(functools.partial(front_kernel, n_tp, n_cp, slice_rows), o...  42.3 us
    ppermute x1, waiting for transfers between devices, local_block(): relay2 = lax.ppermute(relay, 'tp', ring)  14.3 us
    unnamed x7, local copies, waits for them, and re-layouts  7.9 us
  transfers between devices with their start and end apart: 2, of which 1 were waited for; matrix products, arithmetic and copies ran while one was open for 1% of the time, Pallas kernels for 10%

profile of v3, /device:TPU:1, one launch (start us, length us, event | category | flops | bytes accessed | tf_op | source)
XLA Modules:
  0.0 270.6 jit_solution(9968130308955558920)
XLA Ops:
  0.6 1.4 bitcast_reduce_fusion
  2.0 0.7 convert_element_type.3
  2.7 0.1 compare_select_fusion
  2.8 1.7 copy.12.posq_ref
  4.5 3.0 %fusion = (f32[1024,128]{1,0:T(8,128)}, f32[1024,128]{1,0:T(8,128)}) fusion(f32[128]{0:T(128)S(1)} %get-tuple-element.22, f32[128]{0:T(128)S(1)} %get-tuple-element.23, f32[1024]{0:T(1024)S(1)} %convert_element_type.3), kind=kLoop, calls=%fused_computation.2 | loop fusion | flops 262144 | bytes 1053696 | tf_op jit(solution)/shard_map/mul | solution.py:29
  7.6 0.0 copy-start
  7.6 42.3 %front.1 = (bf16[4096,512]{1,0:T(8,128)(2,1)}, s32[3,8,1,128]{3,2,1,0:T(1,128)}, bf16[1024,1024]{1,0:T(8,128)(2,1)}, bf16[64,4096]{1,0:T(8,128)(2,1)}, bf16[2,64,4096]{2,1,0:T(8,128)(2,1)}) custom-call(bf16[1024,4096]{1,0:T(8,128)(2,1)} %x_hbm.3, s32[8,1,128]{2,1,0:T(1,128)} %bitcast.8, f32[1,4096]{1,0:T(1,128)} %bitcast.11, bf16[4096,256]{1,0:T(8,128)(2,1)} %wk_hbm.1, ...), custom_call_target="tpu_custom_call" | custom-call | flops 12884901888 | bytes 25165824 | tf_op jit(solution)/shard_map/front/pallas_call | solution.py:495
  49.9 0.0 copy-done
  49.9 2.5 fusion.1
  52.4 0.0 copy-start.1
  52.4 23.9 %attend.2.oa_hbm = bf16[512,1024]{1,0:T(8,128)(2,1)} custom-call(s32[32]{0:T(128)} %get-tuple-element.14.kmin_ref, s32[32]{0:T(128)} %get-tuple-element.13.kmax_ref, s32[8]{0:T(128)} %get-tuple-element.16.qmin_ref, s32[8]{0:T(128)} %get-tuple-element.15.qmax_ref, bf16[1024,1024]{1,0:T(8,128)(2,1)} %get-tuple-element.9.q_ref, s32[1024,1]{1,0:T(8,128)} %copy.12.posq_ref, ...), custom_call_target="tpu_custom_call" | custom-call | flops 8589934592 | bytes 8388608 | tf_op jit(solution)/shard_map/attend/pallas_call | solution.py:538
  76.3 0.1 collective-permute-start
  76.3 0.0 copy-done.1
  76.3 0.1 collective-permute-start.1
  76.4 1.3 fusion.2
  77.7 0.9 reshape.40
  78.6 0.9 reshape.39
  79.5 27.1 %attend.3.ob_hbm = bf16[512,1024]{1,0:T(8,128)(2,1)} custom-call(s32[32]{0:T(128)} %get-tuple-element.14.kmin_ref, s32[32]{0:T(128)} %get-tuple-element.13.kmax_ref, s32[8]{0:T(128)} %get-tuple-element.16.qmin_ref, s32[8]{0:T(128)} %get-tuple-element.15.qmax_ref, bf16[1024,1024]{1,0:T(8,128)(2,1)} %get-tuple-element.9.q_ref, s32[1024,1]{1,0:T(8,128)} %copy.12.posq_ref, ...), custom_call_target="tpu_custom_call" | custom-call | flops 8589934592 | bytes 8388608 | tf_op jit(solution)/shard_map/attend/pallas_call | solution.py:538
  106.6 0.0 collective-permute-done.la_hbm
  106.6 0.0 copy-start.2
  106.6 14.3 %collective-permute-done.1.relay2_hbm = bf16[2,64,4096]{2,1,0:T(8,128)(2,1)} collective-permute-done((bf16[2,64,4096]{2,1,0:T(8,128)(2,1)S(1)}, bf16[2,64,4096]{2,1,0:T(8,128)(2,1)}, u32[]{:S(2)}, u32[]{:S(2)}) %collective-permute-start.1) | collective-permute-done | bytes 1048608 | tf_op jit(solution)/shard_map/ppermute | solution.py:524
  121.0 0.0 copy-done.2
  121.0 141.8 %out_gather.1 = bf16[1024,4096]{1,0:T(8,128)(2,1)} custom-call(bf16[512,1024]{1,0:T(8,128)(2,1)} %attend.2.oa_hbm, bf16[512,1024]{1,0:T(8,128)(2,1)} %attend.3.ob_hbm, bf16[512,1024]{1,0:T(8,128)(2,1)} %copy-done.2, bf16[1024,4096]{1,0:T(8,128)(2,1)} %w_hbm.1, bf16[64,4096]{1,0:T(8,128)(2,1)} %get-tuple-element.11.wz_hbm, ...), custom_call_target="tpu_custom_call" | custom-call | flops 34359738368 | bytes 50331648 | tf_op jit(solution)/shard_map/out_gather/pallas_call | solution.py:563
  262.8 7.9 %copy.15 = bf16[1024,4096]{1,0:T(8,128)(2,1)} copy(bf16[1024,4096]{1,0:T(8,128)(2,1)} %out_gather.1) | data formatting | bytes 16777216
  (1 shorter events, 0.0 us)
Async XLA Ops:
  7.6 42.3 %copy-start = (s32[1024]{0:T(1024)S(1)}, s32[1024]{0:T(1024)}, u32[]{:S(2)}) copy-start(s32[1024]{0:T(1024)} %param.8) | copy-start | bytes 12292
  52.4 24.0 %copy-start.1 = (bf16[2,64,4096]{2,1,0:T(8,128)(2,1)S(1)}, bf16[2,64,4096]{2,1,0:T(8,128)(2,1)}, u32[]{:S(2)}) copy-start(bf16[2,64,4096]{2,1,0:T(8,128)(2,1)} %get-tuple-element.12.relay_hbm) | copy-start | bytes 3145732
  76.3 30.4 %collective-permute-start = (bf16[512,1024]{1,0:T(8,128)(2,1)}, bf16[512,1024]{1,0:T(8,128)(2,1)S(1)}, u32[]{:S(2)}, u32[]{:S(2)}) collective-permute-start(bf16[512,1024]{1,0:T(8,128)(2,1)} %attend.2.oa_hbm), channel_id=1, source_target_pairs={{0,4},{4,8},{8,12},{12,0},{1,5},{5,9},{9,13},{13,1},{2,6},{6,10},{... | collective-permute-start | bytes 3145736 | tf_op jit(solution)/shard_map/ppermute | solution.py:561
  76.3 44.6 %collective-permute-start.1 = (bf16[2,64,4096]{2,1,0:T(8,128)(2,1)S(1)}, bf16[2,64,4096]{2,1,0:T(8,128)(2,1)}, u32[]{:S(2)}, u32[]{:S(2)}) collective-permute-start(bf16[2,64,4096]{2,1,0:T(8,128)(2,1)S(1)} %copy-done.1), channel_id=1, source_target_pairs={{0,4},{4,8},{8,12},{12,0},{1,5},{5,9},{9,13},{13,1},{2,6},{6,10},{... | collective-permute-start | bytes 3145736 | tf_op jit(solution)/shard_map/ppermute | solution.py:524
  106.6 14.3 %copy-start.2 = (bf16[512,1024]{1,0:T(8,128)(2,1)}, bf16[512,1024]{1,0:T(8,128)(2,1)S(1)}, u32[]{:S(2)}) copy-start(bf16[512,1024]{1,0:T(8,128)(2,1)S(1)} %collective-permute-done.la_hbm) | copy-start | bytes 3145732

commit v4 on v3

--- a/solution.py
+++ b/solution.py
@@ -38,7 +38,7 @@
 FRONT_COLS = 256
 
 
-def front_kernel(n_tp, n_cp, slice_rows, x_hbm, pos_hbm, gain_ref, wk_hbm, wv_hbm, wq_hbm, wo_hbm, cos_ref, sin_ref, kv_hbm, pos_out, q_hbm, wz_hbm, relay_hbm,
+def front_kernel(n_tp, n_cp, slice_rows, x_hbm, pos_hbm, gain_ref, wk_hbm, wv_hbm, wq_hbm, wo_hbm, cos_ref, sin_ref, kv_hbm, pos_out, q_hbm, wz_hbm, wy_hbm, wx_hbm,
                  x_t, normed, wkv, wq_v, kv_t, q_t, x_sem, w_sem, kv_sem, q_sem, p_send, p_recv, s_send, s_recv, z_send, z_recv):
     mesh_id = pl.DeviceIdType.MESH
     tp, dp, cp = lax.axis_index("tp"), lax.axis_index("dp"), lax.axis_index("cp")
@@ -73,8 +73,8 @@
 
     def z_copy(i):
         src, dst = ((wo_hbm.at[pl.ds(pl.multiple_of(own, hs), hs), :], wz_hbm),
-                    (wo_hbm.at[pl.ds(pl.multiple_of(own + hs, hs), hs), :], relay_hbm.at[0]),
-                    (wz_hbm, relay_hbm.at[1]))[i]
+                    (wo_hbm.at[pl.ds(pl.multiple_of(own + hs, hs), hs), :], wy_hbm),
+                    (wz_hbm, wx_hbm))[i]
         return pltpu.make_async_remote_copy(src_ref=src, dst_ref=dst, send_sem=z_send.at[i], recv_sem=z_recv.at[i],
                                             device_id=to_right, device_id_type=mesh_id)
 
@@ -273,11 +273,13 @@
 
 
 TILE = 512
-N_CHUNK = 4
-
-
-def out_kernel(n_tp, n_cp, sl, oa_hbm, ob_hbm, la_hbm, w_hbm, wz_hbm, relay_hbm, relay2_hbm, x_hbm, out_hbm, o_buf, w_buf, acc, w_t, x_t, y_t,
-               o_send, o_recv, w_send, w_recv, w_local, ld_sem, st_sem, own_sem, z_send, z_recv):
+TILE_IN = 256
+N_CHUNK = 8
+A_CHUNKS = 3
+
+
+def out_kernel(n_tp, n_cp, sl, oa_hbm, ob_hbm, la_hbm, w_hbm, wh0, wh1, wh2, wh3, wh4, wh5, x_hbm, out_ref, o_buf, w_buf, acc, w_t, x_t,
+               o_send, o_recv, w_send, w_recv, w_local, ld_sem, own_sem):
     mesh_id = pl.DeviceIdType.MESH
     tp, dp, cp = lax.axis_index("tp"), lax.axis_index("dp"), lax.axis_index("cp")
     core, chip = cp % 2, cp // 2
@@ -286,8 +288,8 @@
     to_x, to_y, to_p = {"dp": 1 - dp}, {"cp": cp_y}, {"cp": cp + 1 - 2 * core}
     p_me, p_x, p_y, p_d = dp * n_cp + cp, (1 - dp) * n_cp + cp, dp * n_cp + cp_y, (1 - dp) * n_cp + cp_y
     n_rows, width = acc.shape
-    half = n_rows // 2
     ch = n_rows // N_CHUNK
+    n_a = A_CHUNKS * ch
     n_tile = width // TILE
     last = n_tp - 1
 
@@ -299,8 +301,8 @@
     def o_copy(s, c):
         at = pl.ds(c * ch, ch)
         if s == 0:
-            src = ob_hbm.at[pl.ds(c * ch - half, ch), :]
-        elif s == 1 and c * ch < half:
+            src = ob_hbm.at[pl.ds(c * ch - n_a, ch), :]
+        elif s == 1 and c < A_CHUNKS:
             src = la_hbm.at[at, :]
         else:
             src = o_buf.at[s, at, :]
@@ -325,19 +327,12 @@
     hs = sl // 2
 
     def w_own_half(k, h):
-        src = ((wz_hbm, relay_hbm.at[0]), (relay_hbm.at[1], relay2_hbm.at[0]), (relay2_hbm.at[1], None))[k][h]
+        src = ((wh0, wh1), (wh2, wh3), (wh4, wh5))[k][h]
         return pltpu.make_async_copy(src, w_buf.at[k, rows(p_me, h * hs, hs), :], w_local.at[k, h])
 
-    def w_last_half():
-        return pltpu.make_async_remote_copy(src_ref=relay2_hbm.at[0], dst_ref=w_buf.at[last - 1, rows(p_me, hs, hs), :], send_sem=z_send,
-                                            recv_sem=z_recv, device_id=to_right, device_id_type=mesh_id)
-
     def start_own(k):
-        w_own_half(k, 0).wait()
-        if k < last - 1:
-            w_own_half(k, 1).wait()
-        else:
-            w_last_half().wait_recv()
+        for h in (0, 1):
+            w_own_half(k, h).wait()
         for kind in ("own_x", "own_y", "own_p"):
             w_copy(k, kind).start()
 
@@ -362,8 +357,8 @@
         if s < last:
             o_copy(s, c).start()
 
-    def tile_cols(t):
-        return pl.ds(pl.multiple_of(t * TILE, TILE), TILE)
+    def tile_cols(t, size=TILE):
+        return pl.ds(pl.multiple_of(t * size, size), size)
 
     def accum(s, r0, r1):
         def body(t, _):
@@ -374,23 +369,19 @@
         lax.fori_loop(0, n_tile, body, 0)
 
     for k in range(last):
-        w_own_half(k, 0).start()
-        if k < last - 1:
-            w_own_half(k, 1).start()
-    for c in (0, 1):
-        o_copy(1, c).start()
-    w_last_half().start()
-    for c in (2, 3):
-        o_copy(0, c).start()
+        for h in (0, 1):
+            w_own_half(k, h).start()
+    for c in range(N_CHUNK):
+        o_copy(1 if c < A_CHUNKS else 0, c).start()
     start_own(0)
-    own = [pltpu.make_async_copy(oa_hbm, o_buf.at[0, pl.ds(0, half), :], own_sem.at[0]),
-           pltpu.make_async_copy(ob_hbm, o_buf.at[0, pl.ds(half, half), :], own_sem.at[1]),
-           pltpu.make_async_copy(la_hbm, o_buf.at[1, pl.ds(0, half), :], own_sem.at[2])]
+    own = [pltpu.make_async_copy(oa_hbm, o_buf.at[0, pl.ds(0, n_a), :], own_sem.at[0]),
+           pltpu.make_async_copy(ob_hbm, o_buf.at[0, pl.ds(n_a, n_rows - n_a), :], own_sem.at[1]),
+           pltpu.make_async_copy(la_hbm, o_buf.at[1, pl.ds(0, n_a), :], own_sem.at[2])]
     for d in own:
         d.start()
 
     def loads(t, slot):
-        cols = tile_cols(t)
+        cols = tile_cols(t, TILE_IN)
         return (pltpu.make_async_copy(w_hbm.at[:, cols], w_t.at[slot], ld_sem.at[slot, 0]),
                 pltpu.make_async_copy(x_hbm.at[:, cols], x_t.at[slot], ld_sem.at[slot, 1]))
 
@@ -402,78 +393,70 @@
     def first(t, _):
         slot = t % 2
 
-        @pl.when(t + 1 < n_tile)
+        @pl.when(t + 1 < width // TILE_IN)
         def _():
             for d in loads(t + 1, (t + 1) % 2):
                 d.start()
 
         for d in loads(t, slot):
             d.wait()
-        acc[:, tile_cols(t)] = x_t[slot].astype(jnp.float32) + jnp.dot(o_buf[0], w_t[slot], preferred_element_type=jnp.float32)
+        acc[:, tile_cols(t, TILE_IN)] = x_t[slot].astype(jnp.float32) + jnp.dot(o_buf[0], w_t[slot], preferred_element_type=jnp.float32)
         return 0
 
-    lax.fori_loop(0, n_tile, first, 0)
-
-    def store(r0, t, slot):
-        return pltpu.make_async_copy(y_t.at[slot], out_hbm.at[pl.ds(r0, ch), tile_cols(t)], st_sem.at[slot])
-
-    def finish(c):
-        r0 = c * ch
-
+    lax.fori_loop(0, width // TILE_IN, first, 0)
+
+    def finish(r0, r1):
         def body(t, _):
-            slot = t % 2
-
-            @pl.when(t >= 2)
-            def _():
-                store(r0, t - 2, slot).wait()
-
             cols = tile_cols(t)
-            y = acc[r0:r0 + ch, cols] + jnp.dot(o_buf[last, r0:r0 + ch, :], w_buf[last - 1, :, cols], preferred_element_type=jnp.float32)
-            y_t[slot] = y.astype(jnp.bfloat16)
-            store(r0, t, slot).start()
+            y = acc[r0:r1, cols] + jnp.dot(o_buf[last, r0:r1, :], w_buf[last - 1, :, cols], preferred_element_type=jnp.float32)
+            out_ref[r0:r1, cols] = y.astype(jnp.bfloat16)
             return 0
 
         lax.fori_loop(0, n_tile, body, 0)
-        store(r0, n_tile - 2, n_tile % 2).wait()
-        store(r0, n_tile - 1, (n_tile - 1) % 2).wait()
 
     pass_on(0)
     start_own(1)
-    arrive(2, 0)
-    arrive(2, 1)
+    for c in range(A_CHUNKS):
+        arrive(2, c)
+    arrive(1, 3)
+    arrive(1, 4)
     pass_diag(0)
-    arrive(1, 2)
+    arrive(1, 5)
     complete(0)
-    accum(1, 0, half)
-    arrive(1, 3)
-    accum(1, half, n_rows)
+    accum(1, 0, 6 * ch)
+    arrive(1, 6)
+    arrive(1, 7)
+    accum(1, 6 * ch, n_rows)
     pass_on(1)
     start_own(2)
-    arrive(3, 0)
     pass_diag(1)
-    arrive(3, 1)
+    arrive(2, 3)
     complete(1)
-    accum(2, 0, half)
-    arrive(2, 2)
+    accum(2, 0, 4 * ch)
+    arrive(2, 4)
+    arrive(2, 5)
+    accum(2, 4 * ch, 6 * ch)
+    arrive(2, 6)
     pass_on(2)
-    arrive(2, 3)
-    accum(2, half, n_rows)
+    arrive(2, 7)
+    accum(2, 6 * ch, n_rows)
     pass_diag(2)
     complete(2)
-    finish(0)
-    finish(1)
-    arrive(3, 2)
-    finish(2)
-    arrive(3, 3)
-    finish(3)
+    for c in range(5):
+        arrive(3, c)
+    finish(0, 5 * ch)
+    arrive(3, 5)
+    arrive(3, 6)
+    finish(5 * ch, 7 * ch)
+    arrive(3, 7)
+    finish(7 * ch, n_rows)
 
     for s in range(last):
         for c in range(N_CHUNK):
-            if s > 0 or c >= 2:
+            if s > 0 or c >= A_CHUNKS:
                 o_copy(s, c).wait_send()
         for kind in ("own_x", "own_y", "own_p", "dx", "dy", "px", "py", "pd0", "pd1"):
             w_copy(s, kind).wait_send()
-    w_last_half().wait_send()
 
 
 def solution(mesh):
@@ -492,13 +475,12 @@
         vmem = pl.BlockSpec(memory_space=pltpu.VMEM)
         pos_row = tok_pos.reshape(rows // KB, 1, KB)
         n_rb = rows // FRONT_ROWS
-        kv_all, pos_far, q_rot, wz, relay = pl.pallas_call(
+        kv_all, pos_far, q_rot, *near = pl.pallas_call(
             functools.partial(front_kernel, n_tp, n_cp, slice_rows),
             out_shape=(jax.ShapeDtypeStruct((n_cp * rows, 2 * k_cols), jnp.bfloat16), jax.ShapeDtypeStruct((n_cp - 1,) + pos_row.shape, jnp.int32),
-                       jax.ShapeDtypeStruct((rows, q_cols), jnp.bfloat16), jax.ShapeDtypeStruct((slice_rows // 2, width), jnp.bfloat16),
-                       jax.ShapeDtypeStruct((2, slice_rows // 2, width), jnp.bfloat16)),
+                       jax.ShapeDtypeStruct((rows, q_cols), jnp.bfloat16), *[jax.ShapeDtypeStruct((slice_rows // 2, width), jnp.bfloat16)] * 3),
             in_specs=[anym, anym, vmem, anym, anym, anym, anym, vmem, vmem],
-            out_specs=(anym,) * 5,
+            out_specs=(anym,) * 6,
             scratch_shapes=[
                 pltpu.VMEM((2, FRONT_ROWS, width), jnp.bfloat16),
                 pltpu.VMEM((rows, width), jnp.bfloat16),
@@ -521,7 +503,9 @@
             cost_estimate=pl.CostEstimate(flops=2 * rows * width * (q_cols + 2 * k_cols), bytes_accessed=24 << 20, transcendentals=0),
             name="front",
         )(hidden, pos_row, norm_gain.reshape(1, width), w_key, w_value, w_query, w_out, cos_tab, sin_tab)
-        relay2 = lax.ppermute(relay, "tp", ring)
+        far_y = lax.ppermute(near[1], "tp", ring)
+        far_x = lax.ppermute(near[2], "tp", ring)
+        far_last = lax.ppermute(far_y, "tp", ring)
         pos_rel = jnp.concatenate([pos_row, pos_far.reshape(-1, 1, KB)], axis=0)
 
         kmin, kmax = jnp.min(pos_rel, axis=(1, 2)), jnp.max(pos_rel, axis=(1, 2))
@@ -530,15 +514,13 @@
         qmin, qmax = jnp.min(qpos, axis=1), jnp.max(qpos, axis=1)
         pos_col = tok_pos.reshape(rows, 1)
 
-        def attend(part, n_parts):
-            steps = n_q // n_parts
-            first = part * steps
+        def attend(first, steps):
             n_rows = (q_cols // HEAD) * QB
             blocks_max = n_cp * rows // KB
             return pl.pallas_call(
                 functools.partial(attn_kernel, first),
                 grid=(steps,),
-                out_shape=jax.ShapeDtypeStruct((rows // n_parts, q_cols), jnp.bfloat16),
+                out_shape=jax.ShapeDtypeStruct((steps * QB, q_cols), jnp.bfloat16),
                 in_specs=[smem] * 4 + [pl.BlockSpec((QB, q_cols), lambda i: (first + i, 0)), pl.BlockSpec((QB, 1), lambda i: (first + i, 0)),
                                        pl.BlockSpec(pos_rel.shape, lambda i: (0, 0, 0)), anym],
                 out_specs=pl.BlockSpec((QB, q_cols), lambda i: (i, 0)),
@@ -553,40 +535,36 @@
                     pltpu.SMEM((blocks_max + WIDE + GROUP,), jnp.int32),
                     pltpu.SemaphoreType.DMA,
                 ],
-                cost_estimate=pl.CostEstimate(flops=4 * rows // n_parts * n_cp * rows * q_cols, bytes_accessed=8 << 20, transcendentals=0),
+                cost_estimate=pl.CostEstimate(flops=4 * steps * QB * n_cp * rows * q_cols, bytes_accessed=8 << 20, transcendentals=0),
                 name="attend",
             )(kmin, kmax, qmin, qmax, q_rot, pos_col, pos_rel, kv_all)
 
-        o_a = attend(0, 2)
+        o_a = attend(0, A_CHUNKS)
         left_a = lax.ppermute(o_a, "tp", ring)
-        o_b = attend(1, 2)
+        o_b = attend(A_CHUNKS, n_q - A_CHUNKS)
         hidden_out = pl.pallas_call(
             functools.partial(out_kernel, n_tp, n_cp, slice_rows),
-            out_shape=jax.ShapeDtypeStruct((rows, width), jnp.bfloat16),
-            in_specs=[anym] * 8,
-            out_specs=anym,
+            out_shape=pltpu.VMEM((rows, width), jnp.bfloat16),
+            in_specs=[anym] * 11,
+            out_specs=vmem,
             scratch_shapes=[
                 pltpu.VMEM((n_tp, rows, q_cols), jnp.bfloat16),
                 pltpu.VMEM((n_tp - 1, q_cols, width), jnp.bfloat16),
                 pltpu.VMEM((rows, width), jnp.float32),
-                pltpu.VMEM((2, q_cols, TILE), jnp.bfloat16),
-                pltpu.VMEM((2, rows, TILE), jnp.bfloat16),
-                pltpu.VMEM((2, rows // N_CHUNK, TILE), jnp.bfloat16),
+                pltpu.VMEM((2, q_cols, TILE_IN), jnp.bfloat16),
+                pltpu.VMEM((2, rows, TILE_IN), jnp.bfloat16),
                 pltpu.SemaphoreType.DMA((n_tp - 1, N_CHUNK)),
                 pltpu.SemaphoreType.DMA((n_tp - 1, N_CHUNK)),
                 pltpu.SemaphoreType.DMA((n_tp - 1, 9)),
                 pltpu.SemaphoreType.DMA((n_tp - 1, 9)),
                 pltpu.SemaphoreType.DMA((n_tp - 1, 2)),
                 pltpu.SemaphoreType.DMA((2, 2)),
-                pltpu.SemaphoreType.DMA((2,)),
                 pltpu.SemaphoreType.DMA((3,)),
-                pltpu.SemaphoreType.DMA,
-                pltpu.SemaphoreType.DMA,
             ],
-            compiler_params=pltpu.CompilerParams(collective_id=0, has_side_effects=True, vmem_limit_bytes=63 << 20),
+            compiler_params=pltpu.CompilerParams(collective_id=0, has_side_effects=True, vmem_limit_bytes=53 << 20),
             cost_estimate=pl.CostEstimate(flops=2 * n_tp * rows * q_cols * width, bytes_accessed=48 << 20, transcendentals=0),
             name="out_gather",
-        )(o_a, o_b, left_a, w_out, wz, relay, relay2, hidden)
+        )(o_a, o_b, left_a, w_out, *near, far_y, far_x, far_last, hidden)
         k_cache = kv_all[:rows, :k_cols].reshape(rows, n_kv, HEAD)
         v_cache = kv_all[:rows, k_cols:].reshape(rows, n_kv, HEAD)
         return hidden_out, k_cache, v_cache

time: 271 us -> 239 us (0.88)
  Pallas kernels: 235 us -> 218 us
  waiting for transfers between devices: 14.3 us -> 0.01 us
  local copies, waits for them, and re-layouts: 12.7 us -> 8.76 us
  starting transfers between devices: 0.12 us -> 3.91 us
    pallas_call x1, Pallas kernels: 142 us -> 125 us  [local_block(): pl.pallas_call(functools.partial(out_kernel, n_tp, n_cp, slice_rows), out...]
    ppermute x1 -> x3, waiting for transfers between devices: 14.3 us -> 0.01 us  [the longest x1 0.01 us: local_block(): far_x = lax.ppermute(near[2], 'tp', ring)]
    unnamed x7 -> x11, local copies, waits for them, and re-layouts: 7.9 us -> 4.61 us
    ppermute x1 -> x3, starting transfers between devices: 0.06 us -> 3.27 us  [the longest x1 3.15 us: local_block(): far_last = lax.ppermute(far_y, 'tp', ring)]
  transfers between devices with their start and end apart: 2 -> 4, of which waited for: 1 -> 0; matrix products, arithmetic and copies ran while one was open for 1% -> 3% of each run, Pallas kernels for 10% -> 21%
where the time goes in v4:
time: 239 us
  Pallas kernels  218 us (91%)
  local copies, waits for them, and re-layouts  8.76 us (4%)
  other arithmetic  6.97 us (3%)
  starting transfers between devices  3.91 us (2%)
    pallas_call x1, Pallas kernels, local_block(): pl.pallas_call(functools.partial(out_kernel, n_tp, n_cp, slice_rows), out...  125 us
    pallas_call x2, Pallas kernels, attend(): pl.pallas_call(functools.partial(attn_kernel, first), grid=(steps,), out_...  50.9 us
    pallas_call x1, Pallas kernels, local_block(): pl.pallas_call(functools.partial(front_kernel, n_tp, n_cp, slice_rows), o...  42.3 us
  transfers between devices with their start and end apart: 4, of which 0 were waited for; matrix products, arithmetic and copies ran while one was open for 3% of the time, Pallas kernels for 21%

profile of v4, /device:TPU:1, one launch (start us, length us, event | category | flops | bytes accessed | tf_op | source)
XLA Modules:
  0.0 238.7 jit_solution(6824598297978934454)
XLA Ops:
  0.6 0.1 compare_select_fusion
  0.7 0.7 convert_element_type.3
  1.4 3.0 %fusion = (f32[1024,128]{1,0:T(8,128)}, f32[1024,128]{1,0:T(8,128)}) fusion(f32[128]{0:T(128)S(1)} %get-tuple-element.24, f32[128]{0:T(128)S(1)} %get-tuple-element.25, f32[1024]{0:T(1024)S(1)} %convert_element_type.3), kind=kLoop, calls=%fused_computation.2 | loop fusion | flops 262144 | bytes 1053696 | tf_op jit(solution)/shard_map/mul | solution.py:29
  4.5 42.3 %front.1 = (bf16[4096,512]{1,0:T(8,128)(2,1)}, s32[3,8,1,128]{3,2,1,0:T(1,128)}, bf16[1024,1024]{1,0:T(8,128)(2,1)}, bf16[64,4096]{1,0:T(8,128)(2,1)}, bf16[64,4...) custom-call(bf16[1024,4096]{1,0:T(8,128)(2,1)} %x_hbm.3, s32[8,1,128]{2,1,0:T(1,128)} %bitcast.7, f32[1,4096]{1,0:T(1,128)} %bitcast.11, ...), custom_call_target="tpu_custom_call" | custom-call | flops 12884901888 | bytes 25165824 | tf_op jit(solution)/shard_map/front/pallas_call | solution.py:478
  46.8 0.1 collective-permute-start.1
  46.8 0.1 collective-permute-start.2
  46.9 0.7 bitcast_reduce_fusion
  47.6 1.0 copy.12.posq_ref
  48.6 2.5 %fusion.1 = (s32[32]{0:T(128)}, s32[32]{0:T(128)}, s32[32,1,128]{2,1,0:T(1,128)}) fusion(s32[24,1,128]{2,1,0:T(1,128)} %bitcast.10, s32[8,1,128]{2,1,0:T(1,128)S(1)} %bitcast.9), kind=kLoop, calls=%fused_computation.9 | loop fusion | flops 12224 | bytes 33024 | tf_op jit(solution)/shard_map/reduce_max | solution.py:511
  51.1 17.9 %attend.2.oa_hbm = bf16[384,1024]{1,0:T(8,128)(2,1)} custom-call(s32[32]{0:T(128)} %get-tuple-element.16.kmin_ref, s32[32]{0:T(128)} %get-tuple-element.15.kmax_ref, s32[8]{0:T(128)} %get-tuple-element.18.qmin_ref, s32[8]{0:T(128)} %get-tuple-element.17.qmax_ref, bf16[1024,1024]{1,0:T(8,128)(2,1)} %get-tuple-element.10.q_ref, s32[1024,1]{1,0:T(8,128)} %copy.12.posq_ref, ...), custom_call_target="tpu_custom_call" | custom-call | flops 6442450944 | bytes 8388608 | tf_op jit(solution)/shard_map/attend/pallas_call | solution.py:520
  69.1 0.6 collective-permute-start
  69.7 1.3 fusion.2
  71.0 0.9 reshape.40
  71.9 0.9 reshape.39
  72.8 0.0 collective-permute-done.1.wh3
  72.8 3.2 %collective-permute-start.3 = (bf16[64,4096]{1,0:T(8,128)(2,1)S(1)}, bf16[64,4096]{1,0:T(8,128)(2,1)S(1)}, u32[]{:S(2)}, u32[]{:S(2)}) collective-permute-start(bf16[64,4096]{1,0:T(8,128)(2,1)S(1)} %collective-permute-done.1.wh3), channel_id=1, source_target_pairs={{0,4},{4,8},{8,12},{12,0},{1,5},{5,9},{9,13},{13,1},{2,6},{6,10},{... | collective-permute-start | bytes 1572872 | tf_op jit(solution)/shard_map/ppermute | solution.py:508
  76.0 32.9 %attend.3.ob_hbm = bf16[640,1024]{1,0:T(8,128)(2,1)} custom-call(s32[32]{0:T(128)} %get-tuple-element.16.kmin_ref, s32[32]{0:T(128)} %get-tuple-element.15.kmax_ref, s32[8]{0:T(128)} %get-tuple-element.18.qmin_ref, s32[8]{0:T(128)} %get-tuple-element.17.qmax_ref, bf16[1024,1024]{1,0:T(8,128)(2,1)} %get-tuple-element.10.q_ref, s32[1024,1]{1,0:T(8,128)} %copy.12.posq_ref, ...), custom_call_target="tpu_custom_call" | custom-call | flops 10737418240 | bytes 8388608 | tf_op jit(solution)/shard_map/attend/pallas_call | solution.py:520
  108.9 0.0 collective-permute-done.2.wh4
  109.0 0.0 collective-permute-done.3.wh5
  109.0 0.7 copy-done.3
  109.7 0.3 copy-done.1
  110.0 0.2 copy-done.4
  110.2 125.1 %out_gather.1 = bf16[1024,4096]{1,0:T(8,128)(2,1)S(1)} custom-call(bf16[384,1024]{1,0:T(8,128)(2,1)} %attend.2.oa_hbm, bf16[640,1024]{1,0:T(8,128)(2,1)} %attend.3.ob_hbm, bf16[384,1024]{1,0:T(8,128)(2,1)} %copy-done.1, bf16[1024,4096]{1,0:T(8,128)(2,1)} %w_hbm.1, bf16[64,4096]{1,0:T(8,128)(2,1)} %get-tuple-element.12.wh0, ...), custom_call_target="tpu_custom_call" | custom-call | flops 34359738368 | bytes 50331648 | tf_op jit(solution)/shard_map/out_gather/pallas_call | solution.py:545
  235.3 3.4 %copy.15 = bf16[1024,4096]{1,0:T(8,128)(2,1)} copy(bf16[1024,4096]{1,0:T(8,128)(2,1)S(1)} %out_gather.1) | data formatting | bytes 16777216
  (9 shorter events, 0.0 us)
Async XLA Ops:
  4.5 42.4 %copy-start = (s32[1024]{0:T(1024)S(1)}, s32[1024]{0:T(1024)}, u32[]{:S(2)}) copy-start(s32[1024]{0:T(1024)} %param.8) | copy-start | bytes 12292
  46.8 26.0 %collective-permute-start.1 = (bf16[64,4096]{1,0:T(8,128)(2,1)}, bf16[64,4096]{1,0:T(8,128)(2,1)S(1)}, u32[]{:S(2)}, u32[]{:S(2)}) collective-permute-start(bf16[64,4096]{1,0:T(8,128)(2,1)} %get-tuple-element.13.wh1), channel_id=1, source_target_pairs={{0,4},{4,8},{8,12},{12,0},{1,5},{5,9},{9,13},{13,1},{2,6},{6,10},{... | collective-permute-start | bytes 1572872 | tf_op jit(solution)/shard_map/ppermute | solution.py:506
  46.8 62.1 %collective-permute-start.2 = (bf16[64,4096]{1,0:T(8,128)(2,1)}, bf16[64,4096]{1,0:T(8,128)(2,1)S(1)}, u32[]{:S(2)}, u32[]{:S(2)}) collective-permute-start(bf16[64,4096]{1,0:T(8,128)(2,1)} %get-tuple-element.14.wh2), channel_id=1, source_target_pairs={{0,4},{4,8},{8,12},{12,0},{1,5},{5,9},{9,13},{13,1},{2,6},{6,10},{... | collective-permute-start | bytes 1572872 | tf_op jit(solution)/shard_map/ppermute | solution.py:507
  69.1 39.9 %collective-permute-start = (bf16[384,1024]{1,0:T(8,128)(2,1)}, bf16[384,1024]{1,0:T(8,128)(2,1)S(1)}, u32[]{:S(2)}, u32[]{:S(2)}) collective-permute-start(bf16[384,1024]{1,0:T(8,128)(2,1)} %attend.2.oa_hbm), channel_id=1, source_target_pairs={{0,4},{4,8},{8,12},{12,0},{1,5},{5,9},{9,13},{13,1},{2,6},{6,10},{... | collective-permute-start | bytes 2359304 | tf_op jit(solution)/shard_map/ppermute | solution.py:543
  72.8 36.1 %copy-start.2 = (bf16[64,4096]{1,0:T(8,128)(2,1)}, bf16[64,4096]{1,0:T(8,128)(2,1)S(1)}, u32[]{:S(2)}) copy-start(bf16[64,4096]{1,0:T(8,128)(2,1)S(1)} %collective-permute-done.1.wh3) | copy-start | bytes 1572868
  72.8 36.2 %collective-permute-start.3 = (bf16[64,4096]{1,0:T(8,128)(2,1)S(1)}, bf16[64,4096]{1,0:T(8,128)(2,1)S(1)}, u32[]{:S(2)}, u32[]{:S(2)}) collective-permute-start(bf16[64,4096]{1,0:T(8,128)(2,1)S(1)} %collective-permute-done.1.wh3), channel_id=1, source_target_pairs={{0,4},{4,8},{8,12},{12,0},{1,5},{5,9},{9,13},{13,1},{2,6},{6,10},{... | collective-permute-start | bytes 1572872 | tf_op jit(solution)/shard_map/ppermute | solution.py:508
  108.9 0.8 copy-start.3
  109.0 1.0 copy-start.1
  109.0 1.2 copy-start.4

commit v5 on v4

--- a/solution.py
+++ b/solution.py
@@ -3,6 +3,7 @@
 
 import jax
 import jax.numpy as jnp
+import numpy as np
 from jax import lax
 from jax.experimental import pallas as pl
 from jax.experimental.pallas import tpu as pltpu
@@ -21,12 +22,9 @@
 QB = 128
 
 
-def rope_tables(tok_pos):
-    inv_freq = 1.0 / (THETA ** (jnp.arange(0, HEAD, 2, dtype=jnp.float32) / HEAD))
-    inv_freq = jnp.concatenate([inv_freq, inv_freq])
-    sign = jnp.where(jnp.arange(HEAD) < HEAD // 2, -1.0, 1.0).astype(jnp.float32)
-    angles = tok_pos.astype(jnp.float32)[:, None] * inv_freq[None, :]
-    return jnp.cos(angles), jnp.sin(angles) * sign[None, :]
+def rope_freqs():
+    freq = (1.0 / (float(THETA) ** (np.arange(0, HEAD, 2) / HEAD))).astype(np.float32)
+    return jnp.asarray(np.concatenate([freq, freq])[None, :])
 
 
 def rotate(x_f32, cos_tab, sin_tab):
@@ -38,8 +36,8 @@
 FRONT_COLS = 256
 
 
-def front_kernel(n_tp, n_cp, slice_rows, x_hbm, pos_hbm, gain_ref, wk_hbm, wv_hbm, wq_hbm, wo_hbm, cos_ref, sin_ref, kv_hbm, pos_out, q_hbm, wz_hbm, wy_hbm, wx_hbm,
-                 x_t, normed, wkv, wq_v, kv_t, q_t, x_sem, w_sem, kv_sem, q_sem, p_send, p_recv, s_send, s_recv, z_send, z_recv):
+def front_kernel(n_tp, n_cp, slice_rows, x_hbm, pos_ref, gain_ref, wk_hbm, wv_hbm, wq_hbm, wo_hbm, freq_ref, kv_hbm, pos_out, q_hbm, wz_hbm, wy_hbm, wx_hbm,
+                 x_t, normed, wkv, wq_v, kv_t, q_t, cos_ref, sin_ref, x_sem, w_sem, kv_sem, q_sem, p_send, p_recv, s_send, s_recv, z_send, z_recv, own_pos_sem):
     mesh_id = pl.DeviceIdType.MESH
     tp, dp, cp = lax.axis_index("tp"), lax.axis_index("dp"), lax.axis_index("cp")
     to_right, to_left = {"tp": (tp + 1) % n_tp}, {"tp": (tp + n_tp - 1) % n_tp}
@@ -81,8 +79,9 @@
     z_copy(0).start()
     z_copy(1).start()
 
-    pos_copies = [pltpu.make_async_remote_copy(src_ref=pos_hbm, dst_ref=pos_out.at[i], send_sem=p_send.at[i], recv_sem=p_recv.at[i],
+    pos_copies = [pltpu.make_async_remote_copy(src_ref=pos_ref, dst_ref=pos_out.at[i + 1], send_sem=p_send.at[i], recv_sem=p_recv.at[i],
                                                device_id=peer, device_id_type=mesh_id) for i, peer in enumerate((to_p, to_y, to_d))]
+    pos_copies.append(pltpu.make_async_copy(pos_ref, pos_out.at[0], own_pos_sem))
     for c in pos_copies:
         c.start()
 
@@ -101,8 +100,18 @@
         send(1, r).start()
         send(0, r).start()
 
+    sign = jnp.where(lax.broadcasted_iota(jnp.int32, (KB, HEAD), 1) < HEAD // 2, -1.0, 1.0).astype(jnp.float32)
+
+    def rope_rows(r):
+        for j in range(r * FRONT_ROWS // KB, (r + 1) * FRONT_ROWS // KB):
+            pos = jnp.transpose(jnp.broadcast_to(pos_ref[j].astype(jnp.float32), (HEAD, KB)))
+            angle = pos * freq_ref[...]
+            cos_ref[j * KB:(j + 1) * KB, :] = jnp.cos(angle)
+            sin_ref[j * KB:(j + 1) * KB, :] = jnp.sin(angle) * sign
+
     for r in range(n_rb):
         at = slice(r * FRONT_ROWS, (r + 1) * FRONT_ROWS)
+        rope_rows(r)
         x_load(r).wait()
         x = x_t[r % 2].astype(jnp.float32)
         var = jnp.mean(x * x, axis=-1, keepdims=True)
@@ -159,7 +168,7 @@
             send(kind, r).wait_send()
 
 
-def attn_kernel(first, kmin_ref, kmax_ref, qmin_ref, qmax_ref, q_ref, posq_ref, posk_ref, kv_hbm, o_ref,
+def attn_kernel(first, kmin_ref, kmax_ref, q_ref, posk_ref, kv_hbm, o_ref,
                 kv_s, q_s, pq_s, m_s, l_s, acc_s, full_l, part_l, sem):
     step = pl.program_id(0)
     n_blocks = kmin_ref.shape[0]
@@ -173,8 +182,8 @@
         load.start()
         load.wait()
 
-    q_lo = qmin_ref[first + step]
-    q_hi = qmax_ref[first + step]
+    q_lo = kmin_ref[first + step]
+    q_hi = kmax_ref[first + step]
 
     def classify(j, counts):
         n_full, n_part = counts
@@ -211,8 +220,9 @@
     for h in range(n_heads):
         q_s[h * QB:(h + 1) * QB, :] = q_ref[:, h * HEAD:(h + 1) * HEAD]
     part_rows = per_kv * QB // PARTS
+    pos_q = jnp.transpose(jnp.broadcast_to(posk_ref[first + step], (HEAD, QB)))
     for h in range(part_rows // QB):
-        pq_s[h * QB:(h + 1) * QB, :] = jnp.broadcast_to(posq_ref[...], (QB, HEAD))
+        pq_s[h * QB:(h + 1) * QB, :] = pos_q
     m_s[...] = jnp.full_like(m_s, NEG_BIG)
     l_s[...] = jnp.zeros_like(l_s)
     acc_s[...] = jnp.zeros_like(acc_s)
@@ -469,17 +479,17 @@
         q_cols, k_cols = w_query.shape[1], w_key.shape[1]
         n_kv = k_cols // HEAD
         slice_rows = w_out.shape[0] // plane
-        cos_tab, sin_tab = rope_tables(tok_pos)
+        freqs = rope_freqs()
         smem = pl.BlockSpec(memory_space=pltpu.SMEM)
         anym = pl.BlockSpec(memory_space=pl.ANY)
         vmem = pl.BlockSpec(memory_space=pltpu.VMEM)
         pos_row = tok_pos.reshape(rows // KB, 1, KB)
         n_rb = rows // FRONT_ROWS
-        kv_all, pos_far, q_rot, *near = pl.pallas_call(
+        kv_all, pos_all, q_rot, *near = pl.pallas_call(
             functools.partial(front_kernel, n_tp, n_cp, slice_rows),
-            out_shape=(jax.ShapeDtypeStruct((n_cp * rows, 2 * k_cols), jnp.bfloat16), jax.ShapeDtypeStruct((n_cp - 1,) + pos_row.shape, jnp.int32),
+            out_shape=(jax.ShapeDtypeStruct((n_cp * rows, 2 * k_cols), jnp.bfloat16), jax.ShapeDtypeStruct((n_cp,) + pos_row.shape, jnp.int32),
                        jax.ShapeDtypeStruct((rows, q_cols), jnp.bfloat16), *[jax.ShapeDtypeStruct((slice_rows // 2, width), jnp.bfloat16)] * 3),
-            in_specs=[anym, anym, vmem, anym, anym, anym, anym, vmem, vmem],
+            in_specs=[anym, vmem, vmem, anym, anym, anym, anym, vmem],
             out_specs=(anym,) * 6,
             scratch_shapes=[
                 pltpu.VMEM((2, FRONT_ROWS, width), jnp.bfloat16),
@@ -488,6 +498,8 @@
                 pltpu.VMEM((width, q_cols), jnp.bfloat16),
                 pltpu.VMEM((n_rb, FRONT_ROWS, 2 * k_cols), jnp.bfloat16),
                 pltpu.VMEM((2, rows, FRONT_COLS), jnp.bfloat16),
+                pltpu.VMEM((rows, HEAD), jnp.float32),
+                pltpu.VMEM((rows, HEAD), jnp.float32),
                 pltpu.SemaphoreType.DMA((2,)),
                 pltpu.SemaphoreType.DMA((3,)),
                 pltpu.SemaphoreType.DMA((n_rb,)),
@@ -498,21 +510,19 @@
                 pltpu.SemaphoreType.DMA((3, n_rb)),
                 pltpu.SemaphoreType.DMA((3,)),
                 pltpu.SemaphoreType.DMA((3,)),
+                pltpu.SemaphoreType.DMA,
             ],
             compiler_params=pltpu.CompilerParams(collective_id=1, has_side_effects=True, vmem_limit_bytes=63 << 20),
             cost_estimate=pl.CostEstimate(flops=2 * rows * width * (q_cols + 2 * k_cols), bytes_accessed=24 << 20, transcendentals=0),
             name="front",
-        )(hidden, pos_row, norm_gain.reshape(1, width), w_key, w_value, w_query, w_out, cos_tab, sin_tab)
+        )(hidden, pos_row, norm_gain.reshape(1, width), w_key, w_value, w_query, w_out, freqs)
         far_y = lax.ppermute(near[1], "tp", ring)
         far_x = lax.ppermute(near[2], "tp", ring)
         far_last = lax.ppermute(far_y, "tp", ring)
-        pos_rel = jnp.concatenate([pos_row, pos_far.reshape(-1, 1, KB)], axis=0)
+        pos_rel = pos_all.reshape(-1, 1, KB)
 
         kmin, kmax = jnp.min(pos_rel, axis=(1, 2)), jnp.max(pos_rel, axis=(1, 2))
         n_q = rows // QB
-        qpos = tok_pos.reshape(n_q, QB)
-        qmin, qmax = jnp.min(qpos, axis=1), jnp.max(qpos, axis=1)
-        pos_col = tok_pos.reshape(rows, 1)
 
         def attend(first, steps):
             n_rows = (q_cols // HEAD) * QB
@@ -521,8 +531,7 @@
                 functools.partial(attn_kernel, first),
                 grid=(steps,),
                 out_shape=jax.ShapeDtypeStruct((steps * QB, q_cols), jnp.bfloat16),
-                in_specs=[smem] * 4 + [pl.BlockSpec((QB, q_cols), lambda i: (first + i, 0)), pl.BlockSpec((QB, 1), lambda i: (first + i, 0)),
-                                       pl.BlockSpec(pos_rel.shape, lambda i: (0, 0, 0)), anym],
+                in_specs=[smem] * 2 + [pl.BlockSpec((QB, q_cols), lambda i: (first + i, 0)), pl.BlockSpec(pos_rel.shape, lambda i: (0, 0, 0)), anym],
                 out_specs=pl.BlockSpec((QB, q_cols), lambda i: (i, 0)),
                 scratch_shapes=[
                     pltpu.VMEM((n_cp * rows, 2 * k_cols), jnp.bfloat16),
@@ -537,7 +546,7 @@
                 ],
                 cost_estimate=pl.CostEstimate(flops=4 * steps * QB * n_cp * rows * q_cols, bytes_accessed=8 << 20, transcendentals=0),
                 name="attend",
-            )(kmin, kmax, qmin, qmax, q_rot, pos_col, pos_rel, kv_all)
+            )(kmin, kmax, q_rot, pos_rel, kv_all)
 
         o_a = attend(0, A_CHUNKS)
         left_a = lax.ppermute(o_a, "tp", ring)

time: 239 us -> 234 us (0.979)
  other arithmetic: 6.97 us -> 1.95 us
    mul x1 -> x0, other arithmetic: 3.04 us -> none  [rope_tables(): return (jnp.cos(angles), jnp.sin(angles) * sign[None, :])]
  transfers between devices with their start and end apart: 4 -> 4, of which waited for: 0 -> 0; matrix products, arithmetic and copies ran while one was open for 3% -> 3% of each run, Pallas kernels for 21% -> 22%
where the time goes in v5:
time: 234 us; the launch traced here: 233 us
  Pallas kernels  218 us (93%)
  local copies, waits for them, and re-layouts  9 us (4%)
  starting transfers between devices  3.93 us (2%)
    pallas_call x1, Pallas kernels, local_block(): pl.pallas_call(functools.partial(out_kernel, n_tp, n_cp, slice_rows), out...  125 us
    pallas_call x2, Pallas kernels, attend(): pl.pallas_call(functools.partial(attn_kernel, first), grid=(steps,), out_...  50.8 us
    pallas_call x1, Pallas kernels, local_block(): pl.pallas_call(functools.partial(front_kernel, n_tp, n_cp, slice_rows), o...  41.8 us
  transfers between devices with their start and end apart: 4, of which 0 were waited for; matrix products, arithmetic and copies ran while one was open for 3% of the time, Pallas kernels for 22%

profile of v5, /device:TPU:1, one launch (start us, length us, event | category | flops | bytes accessed | tf_op | source)
XLA Modules:
  0.0 233.4 jit_solution(6237117095624408243)
XLA Ops:
  0.6 41.8 %front.1 = (bf16[4096,512]{1,0:T(8,128)(2,1)}, s32[4,8,1,128]{3,2,1,0:T(1,128)}, bf16[1024,1024]{1,0:T(8,128)(2,1)}, bf16[64,4096]{1,0:T(8,128)(2,1)}, bf16[64,4...) custom-call(bf16[1024,4096]{1,0:T(8,128)(2,1)} %x_hbm.3, s32[8,1,128]{2,1,0:T(1,128)} %bitcast.6, f32[1,4096]{1,0:T(1,128)} %bitcast.5, ...), custom_call_target="tpu_custom_call" | custom-call | flops 12884901888 | bytes 25165824 | tf_op jit(solution)/shard_map/front/pallas_call | solution.py:488
  42.5 0.1 collective-permute-start.1
  42.5 0.1 collective-permute-start.2
  42.6 1.9 fusion
  44.5 0.7 reduce_max.12.kmax_ref
  45.2 0.6 reduce_min.12.kmin_ref
  45.8 17.9 %attend.2.oa_hbm = bf16[384,1024]{1,0:T(8,128)(2,1)} custom-call(s32[32]{0:T(128)} %reduce_min.12.kmin_ref, s32[32]{0:T(128)} %reduce_max.12.kmax_ref, bf16[1024,1024]{1,0:T(8,128)(2,1)} %get-tuple-element.10.q_ref, s32[32,1,128]{2,1,0:T(1,128)} %bitcast.3, bf16[4096,512]{1,0:T(8,128)(2,1)} %get-tuple-element.11.kv_hbm), custom_call_target="tpu_custom_call" | custom-call | flops 6442450944 | bytes 8388608 | tf_op jit(solution)/shard_map/attend/pallas_call | solution.py:530
  63.8 0.7 collective-permute-start
  64.4 1.3 fusion.1
  65.7 0.9 reshape.27
  66.6 0.9 reshape.26
  67.5 0.0 collective-permute-done.1.wh3
  67.5 3.2 %collective-permute-start.3 = (bf16[64,4096]{1,0:T(8,128)(2,1)S(1)}, bf16[64,4096]{1,0:T(8,128)(2,1)S(1)}, u32[]{:S(2)}, u32[]{:S(2)}) collective-permute-start(bf16[64,4096]{1,0:T(8,128)(2,1)S(1)} %collective-permute-done.1.wh3), channel_id=1, source_target_pairs={{0,4},{4,8},{8,12},{12,0},{1,5},{5,9},{9,13},{13,1},{2,6},{6,10},{... | collective-permute-start | bytes 1572872 | tf_op jit(solution)/shard_map/ppermute | solution.py:521
  70.7 32.9 %attend.3.ob_hbm = bf16[640,1024]{1,0:T(8,128)(2,1)} custom-call(s32[32]{0:T(128)} %reduce_min.12.kmin_ref, s32[32]{0:T(128)} %reduce_max.12.kmax_ref, bf16[1024,1024]{1,0:T(8,128)(2,1)} %get-tuple-element.10.q_ref, s32[32,1,128]{2,1,0:T(1,128)} %bitcast.4, bf16[4096,512]{1,0:T(8,128)(2,1)} %get-tuple-element.11.kv_hbm), custom_call_target="tpu_custom_call" | custom-call | flops 10737418240 | bytes 8388608 | tf_op jit(solution)/shard_map/attend/pallas_call | solution.py:530
  103.6 0.0 copy-done.1
  103.6 0.0 collective-permute-done.2.wh4
  103.6 0.0 copy-start.2
  103.6 0.0 collective-permute-done.la_hbm
  103.6 0.0 collective-permute-done.3.wh5
  103.7 0.7 copy-done.2
  104.4 0.3 copy-done
  104.7 0.2 copy-done.3
  104.9 125.1 %out_gather.1 = bf16[1024,4096]{1,0:T(8,128)(2,1)S(1)} custom-call(bf16[384,1024]{1,0:T(8,128)(2,1)} %attend.2.oa_hbm, bf16[640,1024]{1,0:T(8,128)(2,1)} %attend.3.ob_hbm, bf16[384,1024]{1,0:T(8,128)(2,1)} %copy-done, bf16[1024,4096]{1,0:T(8,128)(2,1)} %w_hbm.1, bf16[64,4096]{1,0:T(8,128)(2,1)} %get-tuple-element.12.wh0, ...), custom_call_target="tpu_custom_call" | custom-call | flops 34359738368 | bytes 50331648 | tf_op jit(solution)/shard_map/out_gather/pallas_call | solution.py:554
  230.0 3.4 %copy.12 = bf16[1024,4096]{1,0:T(8,128)(2,1)} copy(bf16[1024,4096]{1,0:T(8,128)(2,1)S(1)} %out_gather.1) | data formatting | bytes 16777216
  (3 shorter events, 0.0 us)
Async XLA Ops:
  42.5 25.1 %collective-permute-start.1 = (bf16[64,4096]{1,0:T(8,128)(2,1)}, bf16[64,4096]{1,0:T(8,128)(2,1)S(1)}, u32[]{:S(2)}, u32[]{:S(2)}) collective-permute-start(bf16[64,4096]{1,0:T(8,128)(2,1)} %get-tuple-element.13.wh1), channel_id=1, source_target_pairs={{0,4},{4,8},{8,12},{12,0},{1,5},{5,9},{9,13},{13,1},{2,6},{6,10},{... | collective-permute-start | bytes 1572872 | tf_op jit(solution)/shard_map/ppermute | solution.py:519
  42.5 61.1 %collective-permute-start.2 = (bf16[64,4096]{1,0:T(8,128)(2,1)}, bf16[64,4096]{1,0:T(8,128)(2,1)S(1)}, u32[]{:S(2)}, u32[]{:S(2)}) collective-permute-start(bf16[64,4096]{1,0:T(8,128)(2,1)} %get-tuple-element.14.wh2), channel_id=1, source_target_pairs={{0,4},{4,8},{8,12},{12,0},{1,5},{5,9},{9,13},{13,1},{2,6},{6,10},{... | collective-permute-start | bytes 1572872 | tf_op jit(solution)/shard_map/ppermute | solution.py:520
  63.8 39.9 %collective-permute-start = (bf16[384,1024]{1,0:T(8,128)(2,1)}, bf16[384,1024]{1,0:T(8,128)(2,1)S(1)}, u32[]{:S(2)}, u32[]{:S(2)}) collective-permute-start(bf16[384,1024]{1,0:T(8,128)(2,1)} %attend.2.oa_hbm), channel_id=1, source_target_pairs={{0,4},{4,8},{8,12},{12,0},{1,5},{5,9},{9,13},{13,1},{2,6},{6,10},{... | collective-permute-start | bytes 2359304 | tf_op jit(solution)/shard_map/ppermute | solution.py:552
  67.5 36.1 %copy-start.1 = (bf16[64,4096]{1,0:T(8,128)(2,1)}, bf16[64,4096]{1,0:T(8,128)(2,1)S(1)}, u32[]{:S(2)}) copy-start(bf16[64,4096]{1,0:T(8,128)(2,1)S(1)} %collective-permute-done.1.wh3) | copy-start | bytes 1572868
  67.5 36.1 %collective-permute-start.3 = (bf16[64,4096]{1,0:T(8,128)(2,1)S(1)}, bf16[64,4096]{1,0:T(8,128)(2,1)S(1)}, u32[]{:S(2)}, u32[]{:S(2)}) collective-permute-start(bf16[64,4096]{1,0:T(8,128)(2,1)S(1)} %collective-permute-done.1.wh3), channel_id=1, source_target_pairs={{0,4},{4,8},{8,12},{12,0},{1,5},{5,9},{9,13},{13,1},{2,6},{6,10},{... | collective-permute-start | bytes 1572872 | tf_op jit(solution)/shard_map/ppermute | solution.py:521
  103.6 0.8 copy-start.2
  103.6 1.1 copy-start
  103.7 1.2 copy-start.3
